TPU v7x, 256 devices: a whole 4x4x8 slice. The times are simulated.
256 devices in a mesh: dom: 128 (over z, y, x), st: 2 (over core).
Axes of the slice: x: 4, y: 4, z: 8, core: 2. Of those that a mesh axis runs over, the one named last changes fastest.
Arguments:
- psi: float32 [2, 128, 8, 2, 64, 256], P(None, 'dom', None, None, None, 'st'), parts along dimension 5, may hold values from -18 to 18
- potential: float32 [128, 8, 2, 64], P('dom'), may hold values from 0 to 4
Outputs:
- propagated: float32 [2, 128, 8, 2, 64, 256], P(None, 'dom', None, None, None, 'st'), parts along dimension 5
There are 2 independent parts, one for each index of `st`. A program takes and returns all parts, laid end to end along the dimension named above; an argument that names none is the same for every part. Nothing has to cross between parts.
All inputs are finite; a program needn't handle non-finite values.
Results may differ from a plain program's by a relative error of at most 0.0003.
Values sent between devices are 32-bit elements; how exact they have to be, the bound alone decides.
A program may use at most 64 MiB of HBM per device.

v0:
```python
import jax
import jax.numpy as jnp
from jax import lax
from jax.sharding import Mesh
from jax.sharding import PartitionSpec as P

ITERS = 6
DOM = ("dom_0", "dom_1", "dom_2")


epsilon = 1e-06
time_step = 0.5
taylor_terms = 32
far_weight = -1.0 / 12.0
near_weight = 4.0 / 3.0
centre_weight = -7.5


def gather_axes(x, axes, dim):
    out = x
    for number in range(len(axes) - 1, -1, -1):
        out = lax.all_gather(out, axes[number], axis=dim, tiled=True)
    return out


def to_grid(blocked):
    parts, nblocks, cx, by, nz, orbs = blocked.shape
    grid = blocked.transpose(0, 2, 1, 3, 4, 5)
    return grid.reshape(parts, cx, nblocks * by, nz, orbs)


def to_blocks(grid, by):
    parts, nx, ny, nz, orbs = grid.shape
    blocked = grid.reshape(parts, nx, ny // by, by, nz, orbs).transpose(0, 2, 1, 3, 4, 5)
    return blocked


def shift_walls(values, offset):
    width_y = values.shape[2]
    padded = jnp.pad(values, ((0, 0), (0, 0), (2, 2), (0, 0), (0, 0)))
    return padded[:, :, 2 - offset : 2 - offset + width_y]


def hamiltonian_whole(values_in, potential):
    total = centre_weight * values_in
    for along in (1, 3):
        total = total + near_weight * (
            jnp.roll(values_in, 1, along) + jnp.roll(values_in, -1, along)
        )
        total = total + far_weight * (
            jnp.roll(values_in, 2, along) + jnp.roll(values_in, -2, along)
        )
    total = total + near_weight * (shift_walls(values_in, 1) + shift_walls(values_in, -1))
    total = total + far_weight * (shift_walls(values_in, 2) + shift_walls(values_in, -2))
    return -0.5 * total + potential[None, :, :, :, None] * values_in


def tridiagonal(alphas, betas, vector):
    zero_row = jnp.zeros((1, vector.shape[1]), jnp.float32)
    upper = jnp.concatenate([betas * vector[1:], zero_row], axis=0)
    lower = jnp.concatenate([zero_row, betas * vector[:-1]], axis=0)
    return alphas * vector + upper + lower


def krylov_exponential(alphas, betas):
    count = alphas.shape[0]
    first = (jnp.arange(count) == 0).astype(jnp.float32)[:, None] * jnp.ones_like(alphas)
    term_real = first
    term_imag = jnp.zeros_like(alphas)
    sum_real = term_real
    sum_imag = term_imag
    for order in range(1, taylor_terms):
        applied_real = tridiagonal(alphas, betas, term_real)
        applied_imag = tridiagonal(alphas, betas, term_imag)
        term_real = time_step * applied_imag / order
        term_imag = -time_step * applied_real / order
        sum_real = sum_real + term_real
        sum_imag = sum_imag + term_imag
    return (sum_real, sum_imag)


def combine_basis(krylov_basis, alpha_list, beta_list, first_norm):
    coef_real, coef_imag = krylov_exponential(jnp.stack(alpha_list), jnp.stack(beta_list))
    out_real = jnp.zeros_like(krylov_basis[0][0])
    out_imag = jnp.zeros_like(krylov_basis[0][0])
    for index_j in range(len(krylov_basis)):
        basis_now = krylov_basis[index_j]
        out_real = out_real + coef_real[index_j] * basis_now[0] - coef_imag[index_j] * basis_now[1]
        out_imag = out_imag + coef_real[index_j] * basis_now[1] + coef_imag[index_j] * basis_now[0]
    return first_norm * jnp.stack([out_real, out_imag])


def local_lanczos(grid_psi, grid_pot):
    axes_all = (0, 1, 2, 3)
    first_norm = jnp.sqrt(jnp.sum(grid_psi * grid_psi, axis=axes_all) + epsilon)
    vector = grid_psi / first_norm
    previous = jnp.zeros_like(vector)
    beta_prev = jnp.zeros_like(first_norm)
    krylov_basis = []
    alpha_list = []
    beta_list = []
    for iteration in range(ITERS):
        applied = hamiltonian_whole(vector, grid_pot)
        alpha_now = jnp.sum(vector * applied, axis=axes_all)
        krylov_basis.append(vector)
        alpha_list.append(alpha_now)
        if iteration + 1 < ITERS:
            remainder = applied - alpha_now * vector - beta_prev * previous
            beta_now = jnp.sqrt(jnp.sum(remainder * remainder, axis=axes_all) + epsilon)
            previous = vector
            vector = remainder / beta_now
            beta_prev = beta_now
            beta_list.append(beta_now)
    return combine_basis(krylov_basis, alpha_list, beta_list, first_norm)


def on_device(psi, potential):
    by = psi.shape[3]
    moved = lax.all_to_all(psi, DOM, split_axis=5, concat_axis=1, tiled=True)
    whole_pot = gather_axes(potential, DOM, 0)
    grid_pot = to_grid(whole_pot[None, :, :, :, :, None])[0, :, :, :, 0]
    result = to_blocks(local_lanczos(to_grid(moved), grid_pot), by)
    return lax.all_to_all(result, DOM, split_axis=1, concat_axis=5, tiled=True)


def solution(mesh):
    torus = Mesh(mesh.devices.reshape(8, 4, 4, mesh.shape["st"]), ("dom_0", "dom_1", "dom_2", "st"))
    placed = (P(None, DOM, None, None, None, "st"), P(DOM, None, None, None))
    return jax.shard_map(
        on_device,
        mesh=torus,
        in_specs=placed,
        out_specs=P(None, DOM, None, None, None, "st"),
        check_vma=False,
    )
```

profile of v0, /device:TPU:8, one launch (start us, length us, event | category | flops | bytes accessed | tf_op | source)
XLA Modules:
  0.0 239.6 jit_solution(6091869318513850404)
XLA Ops:
  0.0 3.1 %copy.26 = f32[2,1,8,2,64,128]{4,2,3,1,0,5:T(8,128)S(1)} copy(f32[2,1,8,2,64,128]{5,4,3,2,1,0:T(8,128)} %param.2) | data formatting | bytes 2097152 | tf_op args[0]
  3.1 2.3 reshape.90736
  5.4 15.3 %all-to-all-start = ((f32[128,1,2048]{2,1,0:T(1,128)}), f32[128,1,2048]{2,1,0:T(1,128)S(1)}, u32[]{:S(2)}, u32[]{:S(2)}) async-start(f32[128,1,2048]{2,1,0:T(1,128)} %reshape.90736), calls=%async_computation | async-start | bytes 2097152 | tf_op jit(solution)/shard_map/all_to_all | solution.py:119
  20.7 12.4 %all_gather.9 = f32[4,8,2,64]{3,1,2,0:T(8,128)S(1)} all-gather(f32[1,8,2,64]{3,1,2,0:T(8,128)S(1)} %copy.46), channel_id=1, replica_groups=mesh['dom_0'=8,'dom_1'=4,'dom_2'=4,'st'=2] {'dom_2'}, dimensions={0}, use_global_device_ids=true | all-gather | bytes 20480 | tf_op jit(solution)/shard_map/all_gather | solution.py:22
  33.1 12.9 %all_gather.10 = f32[16,8,2,64]{3,1,2,0:T(8,128)S(1)} all-gather(f32[4,8,2,64]{3,1,2,0:T(8,128)S(1)} %all_gather.9), channel_id=1, replica_groups=mesh['dom_0'=8,'dom_1'=4,'dom_2'=4,'st'=2] {'dom_1'}, dimensions={0}, use_global_device_ids=true | all-gather | bytes 81920 | tf_op jit(solution)/shard_map/all_gather | solution.py:22
  46.0 27.7 %all_gather.11 = f32[128,8,2,64]{3,1,2,0:T(8,128)S(1)} all-gather(f32[16,8,2,64]{3,1,2,0:T(8,128)S(1)} %all_gather.10), channel_id=1, replica_groups=mesh['dom_0'=8,'dom_1'=4,'dom_2'=4,'st'=2] {'dom_0'}, dimensions={0}, use_global_device_ids=true | all-gather | bytes 589824 | tf_op jit(solution)/shard_map/all_gather | solution.py:22
  75.3 4.4 %reduce.17 = f32[128,2048]{1,0:T(8,128)} reduce(f32[128,1,2048]{2,1,0:T(1,128)S(1)} %all-to-all-done, f32[]{:T(128)} %broadcast.5502), dimensions={1}, to_apply=%all_to_all.22.reduce_sub_computation | reduce | bytes 2097156 | tf_op jit(solution)/shard_map/all_to_all | solution.py:119
  79.7 2.0 reshape.90737
  81.7 1.2 multiply_reduce_fusion
  83.6 1.8 divide_bitcast_fusion
  85.4 1.6 copy.27
  87.4 2.2 copy.49
  90.5 3.0 %multiply_reduce_fusion.10 = (f32[]{:T(128)}, f32[2,8,256,64,1]{2,3,4,1,0:T(8,128)S(1)}) fusion(f32[2,8,256,64,1]{2,3,4,1,0:T(8,128)S(1)} %copy.49, f32[8,256,64]{1,2,0:T(8,128)S(1)} %copy.47, f32[2,8,256,2,1]{2,3,4,1,0:T(2,128)S(1)} %get-tuple-element.120, f32[2,8,256,62,1]{2,3,4,1,0:T(8,128)S(1)} %get-tuple-element.122, ...), kind=kLoop, calls=%fused_computation.165 | loop fusion | flops 8388607 | bytes 11010052 | tf_op jit(solution)/shard_map/reduce_sum | solution.py:104
  93.6 1.6 multiply_reduce_fusion.9
  95.9 2.0 broadcast_divide_fusion.4
  98.8 3.0 %multiply_reduce_fusion.8 = (f32[]{:T(128)}, f32[2,8,256,64,1]{2,3,4,1,0:T(8,128)S(1)}) fusion(f32[2,8,256,64,1]{2,3,4,1,0:T(8,128)S(1)} %broadcast_divide_fusion.4, f32[8,256,64]{1,2,0:T(8,128)S(1)} %copy.47, f32[2,8,256,2,1]{2,3,4,1,0:T(2,128)S(1)} %get-tuple-element.104, f32[2,8,256,62,1]{2,3,4,1,0:T(8,128)S(1)} %get-tuple-element.106, ...), kind=kLoop, calls=%fused_computation.162 | loop fusion | flops 8388607 | bytes 11010052 | tf_op jit(solution)/shard_map/reduce_sum | solution.py:104
  101.8 2.5 %multiply_reduce_fusion.7 = (f32[]{:T(128)}, f32[2,8,256,64,1]{2,3,4,1,0:T(8,128)}) fusion(f32[2,8,256,64,1]{2,3,4,1,0:T(8,128)S(1)} %copy.49, f32[]{:T(128)} %sqrt.35, f32[2,8,256,64,1]{2,3,4,1,0:T(8,128)S(1)} %get-tuple-element.22, f32[2,8,256,64,1]{2,3,4,1,0:T(8,128)S(1)} %broadcast_divide_fusion.4, f32[]{:T(128)} %get-tuple-element.21), kind=kLoop, calls=%fused_computation.160 | loop fusion | flops 1572863 | bytes 4194316 | tf_op jit(solution)/shard_map/reduce_sum | solution.py:109
  104.9 1.3 broadcast_divide_fusion.3
  107.2 3.1 %multiply_reduce_fusion.6 = (f32[]{:T(128)}, f32[2,8,256,64,1]{2,3,4,1,0:T(8,128)S(1)}) fusion(f32[2,8,256,64,1]{2,3,4,1,0:T(8,128)S(1)} %broadcast_divide_fusion.3, f32[8,256,64]{1,2,0:T(8,128)S(1)} %copy.47, f32[2,8,256,2,1]{2,3,4,1,0:T(2,128)S(1)} %get-tuple-element.88, f32[2,8,256,62,1]{2,3,4,1,0:T(8,128)S(1)} %get-tuple-element.90, ...), kind=kLoop, calls=%fused_computation.159 | loop fusion | flops 8388607 | bytes 11010052 | tf_op jit(solution)/shard_map/reduce_sum | solution.py:104
  110.3 2.6 %multiply_reduce_fusion.5 = (f32[]{:T(128)}, f32[2,8,256,64,1]{2,3,4,1,0:T(8,128)}) fusion(f32[2,8,256,64,1]{2,3,4,1,0:T(8,128)S(1)} %broadcast_divide_fusion.4, f32[]{:T(128)} %sqrt.36, f32[2,8,256,64,1]{2,3,4,1,0:T(8,128)S(1)} %get-tuple-element.18, f32[]{:T(128)} %get-tuple-element.17, f32[2,8,256,64,1]{2,3,4,1,0:T(8,128)S(1)} %copy-done.7), kind=kLoop, calls=%fused_computation.157 | loop fusion | flops 1835007 | bytes 4194316 | tf_op jit(solution)/shard_map/reduce_sum | solution.py:109
  113.6 1.4 broadcast_divide_fusion.2
  116.6 3.2 %multiply_reduce_fusion.4 = (f32[]{:T(128)}, f32[2,8,256,64,1]{2,3,4,1,0:T(8,128)S(1)}) fusion(f32[2,8,256,64,1]{2,3,4,1,0:T(8,128)S(1)} %broadcast_divide_fusion.2, f32[8,256,64]{1,2,0:T(8,128)S(1)} %copy-done.3, f32[2,8,256,2,1]{2,3,4,1,0:T(2,128)S(1)} %get-tuple-element.72, f32[2,8,256,62,1]{2,3,4,1,0:T(8,128)S(1)} %get-tuple-element.74, ...), kind=kLoop, calls=%fused_computation.156 | loop fusion | flops 8388607 | bytes 11010052 | tf_op jit(solution)/shard_map/reduce_sum | solution.py:104
  119.8 2.4 %multiply_reduce_fusion.3 = (f32[]{:T(128)}, f32[2,8,256,64,1]{2,3,4,1,0:T(8,128)}) fusion(f32[]{:T(128)} %sqrt.37, f32[2,8,256,64,1]{2,3,4,1,0:T(8,128)S(1)} %get-tuple-element.14, f32[]{:T(128)} %get-tuple-element.13, f32[2,8,256,64,1]{2,3,4,1,0:T(8,128)S(1)} %copy-done.9, f32[2,8,256,64,1]{2,3,4,1,0:T(8,128)S(1)} %copy-done.8, f32[]{:T(128)} %sqrt.36), kind=kLoop, calls=%fused_computation.154 | loop fusion | flops 2097151 | bytes 4194320 | tf_op jit(solution)/shard_map/reduce_sum | solution.py:109
  122.9 1.3 broadcast_divide_fusion.1
  125.9 2.9 %multiply_reduce_fusion.2 = (f32[]{:T(128)}, f32[2,8,256,64,1]{2,3,4,1,0:T(8,128)S(1)}) fusion(f32[2,8,256,64,1]{2,3,4,1,0:T(8,128)S(1)} %broadcast_divide_fusion.1, f32[8,256,64]{1,2,0:T(8,128)S(1)} %copy-done.4, f32[2,8,256,2,1]{2,3,4,1,0:T(2,128)S(1)} %get-tuple-element.56, f32[2,8,256,62,1]{2,3,4,1,0:T(8,128)S(1)} %get-tuple-element.58, ...), kind=kLoop, calls=%fused_computation.153 | loop fusion | flops 8388607 | bytes 11010052 | tf_op jit(solution)/shard_map/reduce_sum | solution.py:104
  128.9 2.5 %multiply_reduce_fusion.1 = (f32[]{:T(128)}, f32[2,8,256,64,1]{2,3,4,1,0:T(8,128)}) fusion(f32[]{:T(128)} %sqrt.38, f32[2,8,256,64,1]{2,3,4,1,0:T(8,128)S(1)} %get-tuple-element.10, f32[]{:T(128)} %get-tuple-element.9, f32[2,8,256,64,1]{2,3,4,1,0:T(8,128)S(1)} %copy-done.11, f32[2,8,256,64,1]{2,3,4,1,0:T(8,128)S(1)} %copy-done.10, f32[]{:T(128)} %sqrt.37), kind=kLoop, calls=%fused_computation.151 | loop fusion | flops 2097151 | bytes 4194320 | tf_op jit(solution)/shard_map/reduce_sum | solution.py:109
  132.0 1.3 broadcast_divide_fusion
  133.3 1.7 fusion.297
  135.0 1.5 fusion.299
  136.5 1.5 fusion.293
  138.0 1.3 fusion.295
  142.6 1.3 multiply_bitcast_fusion.1
  143.9 7.1 %fusion.98 = f32[]{:T(128)} fusion(f32[2,8,256,64,1]{2,3,4,1,0:T(8,128)} %copy-done.1, f32[2,8,256,2,1]{2,3,4,1,0:T(2,128)} %get-tuple-element.40, f32[2,8,256,62,1]{2,3,4,1,0:T(8,128)} %get-tuple-element.42, f32[2,8,256,62,1]{2,3,4,1,0:T(8,128)} %get-tuple-element.41, f32[2,8,256,2,1]{2,3,4,1,0:T(2,128)} %get-tuple-element.39, ...), kind=kLoop, calls=%fused_computation.166 | loop fusion | flops 8388607 | bytes 9961476 | tf_op jit(solution)/shard_map/reduce_sum | solution.py:104
  151.1 3.9 %stack.56 = f32[6,1]{0,1:T(1,128)S(1)} concatenate(f32[1,1]{0,1:T(1,128)} %bitcast.8, f32[1,1]{0,1:T(1,128)} %bitcast.9, f32[1,1]{0,1:T(1,128)} %bitcast.10, f32[1,1]{0,1:T(1,128)} %bitcast.11, f32[1,1]{0,1:T(1,128)} %bitcast.12, f32[1,1]{0,1:T(1,128)} %bitcast.13), dimensions={0} | concatenate | bytes 48 | tf_op jit(solution)/shard_map/stack | solution.py:83
  162.7 4.3 %multiply_subtract_fusion = (f32[1,8,128,2,64,1]{4,1,3,0,2,5:T(8,128)}, f32[1,8,128,2,64,1]{4,1,3,0,2,5:T(8,128)}) fusion(f32[2,8,128,2,64,1]{4,1,3,0,2,5:T(8,128)} %copy-done.5, f32[]{:T(128)} %bitcast.31, f32[]{:T(128)} %bitcast.27), kind=kLoop, calls=%fused_computation.150 | loop fusion | flops 786432 | bytes 2097160 | tf_op jit(solution)/shard_map/sub | solution.py:88
  167.0 2.3 copy.52
  169.3 9.2 %multiply_subtract_fusion.6 = f32[1,8,256,64,1]{2,3,4,1,0:T(8,128)} fusion(f32[1,8,256,64,1]{2,3,4,1,0:T(8,128)} %copy.52, f32[2,8,256,64,1]{2,3,4,1,0:T(8,128)} %copy-done.1, f32[2,8,256,64,1]{2,3,4,1,0:T(8,128)} %copy-done, f32[2,8,256,64,1]{2,3,4,1,0:T(8,128)S(1)} %broadcast_divide_fusion.2, f32[2,8,256,64,1]{2,3,4,1,0:T(8,128)S(1)} %broadcast_divide_fusion.3, ...), kind=kLoop, calls=%fused_computation.168 | loop fusion | flops 2621440 | bytes 6291496 | tf_op jit(solution)/shard_map/sub | solution.py:88
  178.5 2.4 copy.53
  180.9 2.3 copy.54
  183.2 9.2 %multiply_add_fusion.1 = f32[1,8,256,64,1]{2,3,4,1,0:T(8,128)} fusion(f32[1,8,256,64,1]{2,3,4,1,0:T(8,128)} %copy.54, f32[2,8,256,64,1]{2,3,4,1,0:T(8,128)} %copy-done.1, f32[2,8,256,64,1]{2,3,4,1,0:T(8,128)} %copy-done, f32[2,8,256,64,1]{2,3,4,1,0:T(8,128)S(1)} %broadcast_divide_fusion.2, f32[2,8,256,64,1]{2,3,4,1,0:T(8,128)S(1)} %broadcast_divide_fusion.3, ...), kind=kLoop, calls=%fused_computation.167 | loop fusion | flops 2621440 | bytes 6291496 | tf_op jit(solution)/shard_map/add | solution.py:89
  192.5 2.4 %copy.55 = f32[1,8,256,64,1]{3,1,2,4,0:T(8,128)} copy(f32[1,8,256,64,1]{2,3,4,1,0:T(8,128)} %multiply_add_fusion.1) | data formatting | bytes 1048576 | tf_op jit(solution)/shard_map/add | solution.py:89
  194.9 1.5 copy_bitcast_fusion
  196.5 1.3 reshape.90738
  197.8 32.7 %all_to_all.30 = f32[128,1,2048]{2,1,0:T(1,128)S(1)} all-to-all(f32[128,1,2048]{2,1,0:T(1,128)S(1)} %reshape.90738), channel_id=1, replica_groups=mesh['dom_0'=8,'dom_1'=4,'dom_2'=4,'st'=2] {'dom_0','dom_1','dom_2'}, dimensions={0} | all-to-all | bytes 2097152 | tf_op jit(solution)/shard_map/all_to_all | solution.py:123
  230.5 3.2 %reduce.18 = f32[128,2048]{1,0:T(8,128)S(1)} reduce(f32[128,1,2048]{2,1,0:T(1,128)S(1)} %all_to_all.30, f32[]{:T(128)} %broadcast.5502), dimensions={1}, to_apply=%all_to_all.24.reduce_sub_computation | reduce | bytes 2097156 | tf_op jit(solution)/shard_map/all_to_all | solution.py:123
  233.7 0.8 reshape.90739
  234.5 1.5 bitcast_bitcast_fusion
  236.0 3.6 %copy.57 = f32[2,1,8,2,64,128]{5,4,3,2,1,0:T(8,128)} copy(f32[2,1,8,2,64,128]{4,2,3,0,5,1:T(8,128)} %bitcast_bitcast_fusion) | data formatting | bytes 2097152 | tf_op jit(solution)/shard_map/all_to_all | solution.py:123
  (146 shorter events, 18.8 us)
Async XLA Ops:
  3.1 17.6 %copy-start.14 = (f32[1,8,2,64]{3,2,1,0:T(2,128)S(1)}, f32[1,8,2,64]{3,2,1,0:T(2,128)}, u32[]{:S(2)}) copy-start(f32[1,8,2,64]{3,2,1,0:T(2,128)} %param.3) | copy-start | bytes 12292
  5.4 69.3 %all-to-all-start = ((f32[128,1,2048]{2,1,0:T(1,128)}), f32[128,1,2048]{2,1,0:T(1,128)S(1)}, u32[]{:S(2)}, u32[]{:S(2)}) async-start(f32[128,1,2048]{2,1,0:T(1,128)} %reshape.90736), calls=%async_computation | async-start | bytes 2097152 | tf_op jit(solution)/shard_map/all_to_all | solution.py:119
  74.1 33.1 %copy-start.2 = (f32[8,256,64]{1,2,0:T(8,128)}, f32[8,256,64]{1,2,0:T(8,128)S(1)}, u32[]{:S(2)}) copy-start(f32[8,256,64]{1,2,0:T(8,128)S(1)} %copy.47) | copy-start | bytes 1572868
  81.7 1.9 copy-start.6
  85.4 2.0 copy-start.5
  93.6 2.2 copy-start.12
  107.2 3.1 %copy-start.7 = (f32[2,8,256,64,1]{2,3,4,1,0:T(8,128)S(1)}, f32[2,8,256,64,1]{2,3,4,1,0:T(8,128)}, u32[]{:S(2)}) copy-start(f32[2,8,256,64,1]{2,3,4,1,0:T(8,128)} %get-tuple-element.20) | copy-start | bytes 3145732
  115.5 1.0 copy-start.3
  116.6 3.2 %copy-start.8 = (f32[2,8,256,64,1]{2,3,4,1,0:T(8,128)S(1)}, f32[2,8,256,64,1]{2,3,4,1,0:T(8,128)}, u32[]{:S(2)}) copy-start(f32[2,8,256,64,1]{2,3,4,1,0:T(8,128)} %get-tuple-element.20) | copy-start | bytes 3145732
  116.6 3.2 %copy-start.9 = (f32[2,8,256,64,1]{2,3,4,1,0:T(8,128)S(1)}, f32[2,8,256,64,1]{2,3,4,1,0:T(8,128)}, u32[]{:S(2)}) copy-start(f32[2,8,256,64,1]{2,3,4,1,0:T(8,128)} %get-tuple-element.16) | copy-start | bytes 3145732
  124.2 1.0 copy-start
  124.9 1.0 copy-start.4
  125.9 2.9 %copy-start.10 = (f32[2,8,256,64,1]{2,3,4,1,0:T(8,128)S(1)}, f32[2,8,256,64,1]{2,3,4,1,0:T(8,128)}, u32[]{:S(2)}) copy-start(f32[2,8,256,64,1]{2,3,4,1,0:T(8,128)} %get-tuple-element.16) | copy-start | bytes 3145732
  125.9 2.9 %copy-start.11 = (f32[2,8,256,64,1]{2,3,4,1,0:T(8,128)S(1)}, f32[2,8,256,64,1]{2,3,4,1,0:T(8,128)}, u32[]{:S(2)}) copy-start(f32[2,8,256,64,1]{2,3,4,1,0:T(8,128)} %get-tuple-element.12) | copy-start | bytes 3145732
  133.3 8.1 %copy-start.1 = (f32[2,8,256,64,1]{2,3,4,1,0:T(8,128)}, f32[2,8,256,64,1]{2,3,4,1,0:T(8,128)S(1)}, u32[]{:S(2)}) copy-start(f32[2,8,256,64,1]{2,3,4,1,0:T(8,128)S(1)} %broadcast_divide_fusion) | copy-start | bytes 3145732
  192.5 2.5 %copy-start.13 = (f32[1,8,256,64,1]{3,1,2,4,0:T(8,128)S(1)}, f32[1,8,256,64,1]{3,1,2,4,0:T(8,128)}, u32[]{:S(2)}) copy-start(f32[1,8,256,64,1]{3,1,2,4,0:T(8,128)} %copy.53) | copy-start | bytes 1572868
where the time goes:
time: 241 us; the launch traced here: 240 us
  blocking collectives  85.7 us (36%)
  other arithmetic  84.3 us (35%)
  local copies, waits for them, and re-layouts  49.7 us (21%)
  starting transfers between devices  15.3 us (6%)
  between operations  4.61 us (2%)
    all_gather x3, blocking collectives, gather_axes(): out = lax.all_gather(out, axes[number], axis=dim, tiled=True)  53 us
    all_to_all x1, blocking collectives, on_device(): return lax.all_to_all(result, DOM, split_axis=1, concat_axis=5, tiled=True)  32.7 us
    reduce_sum x6, other arithmetic, local_lanczos(): alpha_now = jnp.sum(vector * applied, axis=axes_all)  22.4 us
    all_to_all x1, starting transfers between devices, on_device(): moved = lax.all_to_all(psi, DOM, split_axis=5, concat_axis=1, tiled=True)  15.3 us
    sub x2, other arithmetic, combine_basis(): out_real + coef_real[index_j] * basis_now[0]  13.5 us
    reduce_sum x5, other arithmetic, local_lanczos(): beta_now = jnp.sqrt(jnp.sum(remainder * remainder, axis=axes_all) + epsilon)  11.6 us
    unnamed x36, local copies, waits for them, and re-layouts  11.3 us
    add x1, other arithmetic, combine_basis(): out_imag + coef_real[index_j] * basis_now[1]  9.23 us
  transfers between devices with their start and end apart: 1, of which 0 were waited for; matrix products, arithmetic and copies ran while one was open for 0% of the time, Pallas kernels for 0%

commit v1 on v0

v1 whole, which is shorter than its diff:
```python
import jax
import jax.numpy as jnp
from jax import lax
from jax.experimental import pallas as pl
from jax.experimental.pallas import tpu as pltpu
from jax.sharding import Mesh
from jax.sharding import PartitionSpec as P

MESH = pl.DeviceIdType.MESH
ITERS = 6
TERMS = 32
EPS = 1e-6
STEP = 0.5
SHIFT = 6.0
RADIUS = 6.0
HALO = 6
NX, NY, NZ = 4, 4, 8
PLANE = NX * NY
SLABS = PLANE + 2 * HALO
CHUNKS = 2
OFFSETS = (
    (2, 2), (2, 1), (1, 2), (2, 3), (3, 2), (1, 1), (3, 3), (1, 3), (3, 1),
    (2, 0), (0, 2), (1, 0), (0, 1), (3, 0), (0, 3),
)


def lanczos_weights(moments):
    first_norm = jnp.sqrt(moments[0] + EPS)
    inverse = 1.0 / first_norm
    sig = [value * inverse for value in moments]
    coef = [inverse]
    sig_prev, coef_prev, beta_prev = None, None, None
    alphas, betas, basis = [], [], []
    for j in range(ITERS):
        count = 2 * ITERS - 1 - j
        shifted = [0.5 * RADIUS * (sig[l + 1] + sig[abs(l - 1)]) for l in range(count)]
        alpha = coef[0] * (SHIFT * sig[0] + shifted[0])
        for k in range(1, j + 1):
            alpha = alpha + coef[k] * (SHIFT * sig[k] + shifted[k])
        alpha = jnp.clip(alpha, 0.0, 12.0)
        alphas.append(alpha)
        basis.append(coef)
        if j + 1 == ITERS:
            break
        rest = SHIFT - alpha
        r_sig = [shifted[l] + rest * sig[l] for l in range(count)]
        if j:
            r_sig = [r_sig[l] - beta_prev * sig_prev[l] for l in range(count)]
        r_coef = []
        for k in range(j + 2):
            terms = []
            if k >= 1:
                terms.append((RADIUS if k == 1 else 0.5 * RADIUS) * coef[k - 1])
            if k + 1 <= j:
                terms.append(0.5 * RADIUS * coef[k + 1])
            if k <= j:
                terms.append(rest * coef[k])
            if j and k < j:
                terms.append(-(beta_prev * coef_prev[k]))
            total = terms[0]
            for term in terms[1:]:
                total = total + term
            r_coef.append(total)
        square = r_coef[0] * r_sig[0]
        for k in range(1, j + 2):
            square = square + r_coef[k] * r_sig[k]
        beta = jnp.sqrt(jnp.clip(square, 0.0, 36.5) + EPS)
        betas.append(beta)
        scale = 1.0 / beta
        sig_prev, coef_prev, beta_prev = sig, coef, beta
        sig = [jnp.clip(value * scale, -first_norm, first_norm) for value in r_sig]
        coef = [value * scale for value in r_coef]
    zero = jnp.zeros_like(first_norm)
    term = [zero + 1.0] + [zero] * (ITERS - 1)
    sums = [list(term), [zero] * ITERS]
    for order in range(1, TERMS):
        factor = STEP / order if order % 2 == 0 else -STEP / order
        applied = []
        for i in range(ITERS):
            value = alphas[i] * term[i]
            if i + 1 < ITERS:
                value = value + betas[i] * term[i + 1]
            if i:
                value = value + betas[i - 1] * term[i - 1]
            applied.append(factor * value)
        term = applied
        sums[order % 2] = [a + b for a, b in zip(sums[order % 2], term)]
    weights = []
    for part in range(2):
        row = []
        for k in range(ITERS):
            total = sums[part][k] * basis[k][k]
            for j in range(k + 1, ITERS):
                total = total + sums[part][j] * basis[j][k]
            row.append(first_norm * total)
        weights.append(row)
    return weights


def kernel(psi, pot, out, snd, own_pot, pots, u0, us, outs, back, mixed, gram, *sems):
    (pot_send, pot_recv, pot_halo_send, pot_halo_recv, in_send, in_recv, halo_send, halo_recv,
     gram_send, gram_recv, out_send, out_recv) = sems
    z, y, x, st = (lax.axis_index(name) for name in ("dom_0", "dom_1", "dom_2", "st"))
    me = y * NX + x
    lane = lax.broadcasted_iota(jnp.int32, (8, 128), 1)
    sub = lax.broadcasted_iota(jnp.int32, (8, 128), 0)

    def at(offset):
        to_y = lax.rem(y + offset[0], NY)
        to_x = lax.rem(x + offset[1], NX)
        return to_y * NX + to_x, (z, to_y, to_x, st)

    barrier = pltpu.get_barrier_semaphore()
    for offset in OFFSETS:
        pl.semaphore_signal(barrier, inc=1, device_id=at(offset)[1], device_id_type=MESH)
    for dz in range(1, NZ):
        pl.semaphore_signal(barrier, inc=1, device_id=(lax.rem(z + dz, NZ), y, x, st), device_id_type=MESH)

    for j in range(2):
        tile = jnp.concatenate([pot[0:4, j, :], pot[4:8, j, :]], axis=1)
        own_pot[4 * j : 4 * j + 4, :] = tile
    pots[HALO + me] = own_pot[...]

    wide = lax.broadcasted_iota(jnp.int32, (128, 128), 1)
    low = lax.rem(wide, 8) < 4

    def to_peers(chunk):
        for j in range(2):
            for i in range(4):
                re = jnp.concatenate([psi[0, i, j], psi[0, i + 4, j]], axis=0)
                im = jnp.concatenate([psi[1, i, j], psi[1, i + 4, j]], axis=0)
                if chunk == 0:
                    both = jnp.where(low, re, pltpu.roll(im, 4, 1))
                else:
                    both = jnp.where(low, pltpu.roll(re, 124, 1), im)
                snd[chunk, :, j, i] = both.T.reshape(PLANE, 8, 128)

    def send_in(chunk):
        for number, offset in enumerate(OFFSETS):
            peer, where = at(offset)
            pltpu.make_async_remote_copy(
                src_ref=snd.at[chunk, peer], dst_ref=u0.at[chunk, HALO + me],
                send_sem=in_send.at[chunk, number], recv_sem=in_recv.at[chunk, me],
                device_id=where, device_id_type=MESH,
            ).start()

    to_peers(0)
    pl.semaphore_wait(barrier, len(OFFSETS) + NZ - 1)
    for number, offset in enumerate(OFFSETS):
        peer, where = at(offset)
        pltpu.make_async_remote_copy(
            src_ref=own_pot, dst_ref=pots.at[HALO + me],
            send_sem=pot_send.at[number], recv_sem=pot_recv.at[me],
            device_id=where, device_id_type=MESH,
        ).start()
    send_in(0)
    to_peers(1)
    send_in(1)
    for chunk in range(CHUNKS):
        u0[chunk, HALO + me] = snd[chunk, me]

    has_low, has_high = z > 0, z < NZ - 1
    below, above = (jnp.maximum(z - 1, 0), y, x, st), (jnp.minimum(z + 1, NZ - 1), y, x, st)

    @pl.when(jnp.logical_not(has_low))
    def _():
        for chunk in range(CHUNKS):
            u0[chunk, 0:HALO] = jnp.zeros((HALO,) + u0.shape[2:], jnp.float32)
        pots[0:HALO] = jnp.zeros((HALO, 8, 128), jnp.float32)

    @pl.when(jnp.logical_not(has_high))
    def _():
        for chunk in range(CHUNKS):
            u0[chunk, HALO + PLANE : SLABS] = jnp.zeros((HALO,) + u0.shape[2:], jnp.float32)
        pots[HALO + PLANE : SLABS] = jnp.zeros((HALO, 8, 128), jnp.float32)

    def wait_recv(ref, sem):
        pltpu.make_async_remote_copy(
            src_ref=ref, dst_ref=ref, send_sem=sem, recv_sem=sem,
            device_id=(z, y, x, st), device_id_type=MESH,
        ).wait_recv()

    def wait_send(ref, sem):
        pltpu.make_async_remote_copy(
            src_ref=ref, dst_ref=ref, send_sem=sem, recv_sem=sem,
            device_id=(z, y, x, st), device_id_type=MESH,
        ).wait_send()

    def halo_copy(chunk, slot, up):
        source = PLANE + slot if up else HALO + slot
        target = slot if up else HALO + PLANE + slot
        return pltpu.make_async_remote_copy(
            src_ref=u0.at[chunk, source], dst_ref=u0.at[chunk, target],
            send_sem=halo_send.at[chunk, int(up), slot], recv_sem=halo_recv.at[chunk, int(up), slot],
            device_id=above if up else below, device_id_type=MESH,
        )

    def pot_halo_copy(up):
        source = PLANE if up else HALO
        target = 0 if up else HALO + PLANE
        return pltpu.make_async_remote_copy(
            src_ref=pots.at[pl.ds(source, HALO)], dst_ref=pots.at[pl.ds(target, HALO)],
            send_sem=pot_halo_send.at[int(up)], recv_sem=pot_halo_recv.at[int(up)],
            device_id=above if up else below, device_id_type=MESH,
        )

    def forward(chunk):
        for p in range(PLANE):
            @pl.when(me != p)
            def _():
                wait_recv(u0.at[chunk, HALO + p], in_recv.at[chunk, p])
            if p < HALO:
                @pl.when(has_low)
                def _():
                    halo_copy(chunk, p, False).start()
            if p >= PLANE - HALO:
                @pl.when(has_high)
                def _():
                    halo_copy(chunk, p - PLANE + HALO, True).start()

    for p in range(PLANE):
        @pl.when(me != p)
        def _():
            wait_recv(pots.at[HALO + p], pot_recv.at[p])

    @pl.when(has_low)
    def _():
        pot_halo_copy(False).start()

    @pl.when(has_high)
    def _():
        pot_halo_copy(True).start()

    for chunk in range(CHUNKS):
        forward(chunk)

    @pl.when(has_low)
    def _():
        pot_halo_copy(True).wait_recv()

    @pl.when(has_high)
    def _():
        pot_halo_copy(False).wait_recv()

    low_mask = jnp.where(has_low, 1.0, 0.0)
    high_mask = jnp.where(has_high, 1.0, 0.0)
    half = lane & 64
    spot = lane & 63
    shifts = [half | ((spot + d) & 63) for d in (-1, 1, -2, 2)]

    def pick(value, index):
        return jnp.take_along_axis(value, index, axis=1, mode="promise_in_bounds")

    centre = (3.75 - SHIFT) * (2.0 / RADIUS)
    near_w = -(2.0 / 3.0) * (2.0 / RADIUS)
    far_w = (1.0 / 24.0) * (2.0 / RADIUS)

    def apply(chunk, k, b, mask):
        size = 0.5 if k == 0 else 1.0
        source = (lambda s, j, i: u0[chunk, s, j, i]) if k == 0 else (lambda s, j, i: us[chunk, k - 1, s, j, i])
        before = [[source(b - 1, j, i) for i in range(4)] for j in range(2)]
        here = [[source(b, j, i) for i in range(4)] for j in range(2)]
        after = [[source(b + 1, j, i) for i in range(4)] for j in range(2)]
        rows = [before[0], before[1], here[0], here[1], after[0], after[1]]
        values, results = [], []
        for j in range(2):
            row = rows[2 + j]
            swap = [pltpu.roll(v, 64, 1) for v in row]
            ring = [swap[2], swap[3]] + row + [swap[0], swap[1]]
            for i in range(4):
                v = row[i]
                zs = [pick(v, index) for index in shifts]
                near = (ring[i + 1] + ring[i + 3]) + (rows[1 + j][i] + rows[3 + j][i]) + (zs[0] + zs[1])
                far = (ring[i] + ring[i + 4]) + (rows[j][i] + rows[4 + j][i]) + (zs[2] + zs[3])
                weight = (2.0 / RADIUS * size) * pots[b, pl.ds(4 * j + i, 1), :] + centre * size
                new = weight * v + ((near_w * size) * near + (far_w * size) * far)
                if k == 1:
                    new = new - u0[chunk, b, j, i]
                elif k > 1:
                    new = new - us[chunk, k - 2, b, j, i]
                if mask is not None:
                    new = new * mask
                values.append(v)
                results.append(new)
                if k + 1 < ITERS:
                    us[chunk, k, b, j, i] = new
        return values, results

    def tree(values):
        while len(values) > 1:
            values = [values[i] + values[i + 1] for i in range(0, len(values) - 1, 2)] + (
                [values[-1]] if len(values) % 2 else []
            )
        return values[0]

    zero = jnp.zeros((8, 128), jnp.float32)

    def moments_of(chunk):
        pairs = []
        for k in range(ITERS):
            def low_body(b, carry):
                apply(chunk, k, b, low_mask)
                return carry

            def high_body(b, carry):
                apply(chunk, k, b, high_mask)
                return carry

            def own_body(b, carry):
                values, results = apply(chunk, k, b, None)
                same = tree([v * v for v in values])
                next_ = tree([v * r for v, r in zip(values, results)])
                return carry[0] + same, carry[1] + next_

            if k + 1 < ITERS:
                lax.fori_loop(1 + k, HALO, low_body, 0)
                lax.fori_loop(HALO + PLANE, SLABS - 1 - k, high_body, 0)
            pairs.append(lax.fori_loop(HALO, HALO + PLANE, own_body, (zero, zero)))
        tile = zero
        for k, pair in enumerate(pairs):
            for odd in range(2):
                total = jnp.sum(pair[odd], axis=1, keepdims=True)
                tile = jnp.where(lane == 2 * k + odd, total, tile)
        return tile

    def send_gram(chunk):
        for dz in range(1, NZ):
            pltpu.make_async_remote_copy(
                src_ref=gram.at[chunk, z], dst_ref=gram.at[chunk, z],
                send_sem=gram_send.at[chunk, dz], recv_sem=gram_recv.at[chunk, z],
                device_id=(lax.rem(z + dz, NZ), y, x, st), device_id_type=MESH,
            ).start()

    for chunk in range(CHUNKS):
        for slot in range(HALO):
            @pl.when(has_low)
            def _():
                halo_copy(chunk, slot, True).wait_recv()

            @pl.when(has_high)
            def _():
                halo_copy(chunk, slot, False).wait_recv()
        gram[chunk, z] = moments_of(chunk)
        send_gram(chunk)

    def finish(chunk):
        for p in range(NZ):
            @pl.when(z != p)
            def _():
                wait_recv(gram.at[chunk, p], gram_recv.at[chunk, p])
        total = tree([gram[chunk, p] for p in range(NZ)])
        total = total + pltpu.roll(total, 4, 0)
        raw = [jnp.broadcast_to(total[:, l : l + 1], (8, 128)) for l in range(2 * ITERS)]
        moments = raw[:2] + [2.0 * raw[l] - raw[l % 2] for l in range(2, 2 * ITERS)]
        real, imag = lanczos_weights(moments)
        imag = [jnp.where(sub < 4, value, -value) for value in imag]

        def combine(q, carry):
            for j in range(2):
                for i in range(4):
                    v = u0[chunk, HALO + q, j, i]
                    straight, crossed = real[0] * v, imag[0] * v
                    for k in range(1, ITERS):
                        v = us[chunk, k - 1, HALO + q, j, i]
                        straight = straight + real[k] * v
                        crossed = crossed + imag[k] * v
                    outs[chunk, q, j, i] = straight + pltpu.roll(crossed, 4, 0)
            return carry

        lax.fori_loop(0, PLANE, combine, 0)
        for number, offset in enumerate(OFFSETS):
            peer, where = at(offset)
            pltpu.make_async_remote_copy(
                src_ref=outs.at[chunk, peer], dst_ref=back.at[chunk, me],
                send_sem=out_send.at[chunk, number], recv_sem=out_recv.at[chunk, me],
                device_id=where, device_id_type=MESH,
            ).start()
        back[chunk, me] = outs[chunk, me]

    for chunk in range(CHUNKS):
        finish(chunk)

    for chunk in range(CHUNKS):
        for p in range(PLANE):
            @pl.when(me != p)
            def _():
                wait_recv(back.at[chunk, p], out_recv.at[chunk, p])
        for j in range(2):
            for i in range(4):
                cells = back[chunk, :, j, i].reshape(128, 128).T
                if chunk == 0:
                    mixed[j, i] = cells
                else:
                    first = mixed[j, i]
                    re = jnp.where(low, first, pltpu.roll(cells, 4, 1))
                    im = jnp.where(low, pltpu.roll(first, 124, 1), cells)
                    out[0, i, j] = re[0:64]
                    out[0, i + 4, j] = re[64:128]
                    out[1, i, j] = im[0:64]
                    out[1, i + 4, j] = im[64:128]

    for number in range(len(OFFSETS)):
        wait_send(own_pot, pot_send.at[number])
        for chunk in range(CHUNKS):
            wait_send(snd.at[chunk, 0], in_send.at[chunk, number])
            wait_send(outs.at[chunk, 0], out_send.at[chunk, number])
    for chunk in range(CHUNKS):
        for dz in range(1, NZ):
            wait_send(gram.at[chunk, 0], gram_send.at[chunk, dz])

    @pl.when(has_low)
    def _():
        pot_halo_copy(False).wait_send()
        for chunk in range(CHUNKS):
            for slot in range(HALO):
                halo_copy(chunk, slot, False).wait_send()

    @pl.when(has_high)
    def _():
        pot_halo_copy(True).wait_send()
        for chunk in range(CHUNKS):
            for slot in range(HALO):
                halo_copy(chunk, slot, True).wait_send()


def on_device(psi, potential):
    parts, _, cx, by, nz, orbs = psi.shape
    dma = pltpu.SemaphoreType.DMA
    peers = len(OFFSETS)
    tiles = (2, 4, 8, 128)
    result = pl.pallas_call(
        kernel,
        out_shape=jax.ShapeDtypeStruct((parts, cx, by, nz, orbs), jnp.float32),
        in_specs=[pl.BlockSpec(memory_space=pltpu.VMEM)] * 2,
        out_specs=pl.BlockSpec(memory_space=pltpu.VMEM),
        scratch_shapes=[
            pltpu.VMEM((CHUNKS, PLANE) + tiles, jnp.float32),
            pltpu.VMEM((8, 128), jnp.float32),
            pltpu.VMEM((SLABS, 8, 128), jnp.float32),
            pltpu.VMEM((CHUNKS, SLABS) + tiles, jnp.float32),
            pltpu.VMEM((CHUNKS, ITERS - 1, SLABS) + tiles, jnp.float32),
            pltpu.VMEM((CHUNKS, PLANE) + tiles, jnp.float32),
            pltpu.VMEM((CHUNKS, PLANE) + tiles, jnp.float32),
            pltpu.VMEM((2, 4, 128, 128), jnp.float32),
            pltpu.VMEM((CHUNKS, NZ, 8, 128), jnp.float32),
            dma((peers,)), dma((PLANE,)), dma((2,)), dma((2,)),
            dma((CHUNKS, peers)), dma((CHUNKS, PLANE)),
            dma((CHUNKS, 2, HALO)), dma((CHUNKS, 2, HALO)),
            dma((CHUNKS, NZ)), dma((CHUNKS, NZ)),
            dma((CHUNKS, peers)), dma((CHUNKS, PLANE)),
        ],
        compiler_params=pltpu.CompilerParams(
            collective_id=0, has_side_effects=True, vmem_limit_bytes=48 * 1024 * 1024
        ),
    )(psi.reshape(parts, cx, by, nz, orbs), potential.reshape(cx, by, nz))
    return result.reshape(psi.shape)


def solution(mesh):
    names = ("dom_0", "dom_1", "dom_2", "st")
    torus = Mesh(mesh.devices.reshape(NZ, NY, NX, mesh.shape["st"]), names)
    placed = (P(None, names[:3], None, None, None, "st"), P(names[:3], None, None, None))
    return jax.shard_map(
        on_device,
        mesh=torus,
        in_specs=placed,
        out_specs=P(None, names[:3], None, None, None, "st"),
        check_vma=False,
    )
```

time: 241 us -> 88.7 us (0.37)
  Pallas kernels: 0 us -> 85.7 us
  blocking collectives: 85.7 us -> 0 us
  other arithmetic: 84.3 us -> 0 us
  local copies, waits for them, and re-layouts: 49.7 us -> 2.89 us
  starting transfers between devices: 15.3 us -> 0 us
  between operations: 4.61 us -> 0.01 us
    pallas_call x0 -> x1, Pallas kernels: none -> 85.7 us  [on_device(): pl.pallas_call(kernel, out_shape=jax.ShapeDtypeStruct((parts, cx, by, nz,...]
    all_gather x3 -> x0, blocking collectives: 53 us -> none  [gather_axes(): out = lax.all_gather(out, axes[number], axis=dim, tiled=True)]
    reduce_sum x12 -> x0, other arithmetic: 35.1 us -> none  [the longest x6 22.4 us: local_lanczos(): alpha_now = jnp.sum(vector * applied, axis=axes_all)]
    all_to_all x1 -> x0, blocking collectives: 32.7 us -> none  [on_device(): return lax.all_to_all(result, DOM, split_axis=1, concat_axis=5, tiled=True)]
    all_to_all x1 -> x0, starting transfers between devices: 15.3 us -> none  [on_device(): moved = lax.all_to_all(psi, DOM, split_axis=5, concat_axis=1, tiled=True)]
    slice x50 -> x0, local copies, waits for them, and re-layouts: 14.4 us -> none  [the longest x24 6.68 us: hamiltonian_whole(): jnp.roll(values_in, 1, along) + jnp.roll(values_in, -1, along)]
    sub x2 -> x0, other arithmetic: 13.5 us -> none  [combine_basis(): out_real + coef_real[index_j] * basis_now[0]]
    div x34 -> x0, other arithmetic: 11.4 us -> none  [the longest x5 7.35 us: local_lanczos(): vector = remainder / beta_now]
  transfers between devices with their start and end apart: 1 -> 0, of which waited for: 0 -> 0; matrix products, arithmetic and copies ran while one was open for 0% -> 0% of each run, Pallas kernels for 0% -> 0%
where the time goes in v1:
time: 88.7 us; the launch traced here: 88.6 us
  Pallas kernels  85.7 us (97%)
  local copies, waits for them, and re-layouts  2.89 us (3%)
    pallas_call x1, Pallas kernels, on_device(): pl.pallas_call(kernel, out_shape=jax.ShapeDtypeStruct((parts, cx, by, nz,...  85.7 us
    unnamed x5, local copies, waits for them, and re-layouts  2.89 us

profile of v1, /device:TPU:8, one launch (start us, length us, event | category | flops | bytes accessed | tf_op | source)
XLA Modules:
  0.0 88.6 jit_solution(16906927258180944122)
XLA Ops:
  0.0 0.0 copy-start
  0.0 1.2 %copy-done = f32[2,1,8,2,64,128]{5,4,3,2,1,0:T(8,128)S(1)} copy-done((f32[2,1,8,2,64,128]{5,4,3,2,1,0:T(8,128)S(1)}, f32[2,1,8,2,64,128]{5,4,3,2,1,0:T(8,128)}, u32[]{:S(2)}) %copy-start) | copy-done | bytes 1048600
  1.2 0.0 copy-start.1
  1.2 0.7 copy-done.1
  1.9 85.7 %shard_map.28 = f32[2,8,2,64,128]{4,3,2,1,0:T(8,128)S(1)} custom-call(f32[2,8,2,64,128]{4,3,2,1,0:T(8,128)S(1)} %bitcast.6, f32[8,2,64]{2,1,0:T(2,128)S(1)} %bitcast.7), custom_call_target="tpu_custom_call" | custom-call | tf_op jit(solution)/shard_map/pallas_call | solution.py:431
  87.6 1.0 %copy.5 = f32[2,1,8,2,64,128]{5,4,3,2,1,0:T(8,128)} copy(f32[2,1,8,2,64,128]{5,4,3,2,1,0:T(8,128)S(1)} %bitcast.5) | data formatting | bytes 2097152
Async XLA Ops:
  0.0 1.2 %copy-start = (f32[2,1,8,2,64,128]{5,4,3,2,1,0:T(8,128)S(1)}, f32[2,1,8,2,64,128]{5,4,3,2,1,0:T(8,128)}, u32[]{:S(2)}) copy-start(f32[2,1,8,2,64,128]{5,4,3,2,1,0:T(8,128)} %param.2) | copy-start | bytes 3145732
  1.2 0.7 copy-start.1

commit v2 on v1

--- a/solution.py
+++ b/solution.py
@@ -18,6 +18,7 @@
 PLANE = NX * NY
 SLABS = PLANE + 2 * HALO
 CHUNKS = 2
+GROUP = 4
 OFFSETS = (
     (2, 2), (2, 1), (1, 2), (2, 3), (3, 2), (1, 1), (3, 3), (1, 3), (3, 1),
     (2, 0), (0, 2), (1, 0), (0, 1), (3, 0), (0, 3),
@@ -97,8 +98,9 @@
     return weights
 
 
-def kernel(psi, pot, out, snd, own_pot, pots, u0, us, outs, back, mixed, gram, *sems):
-    (pot_send, pot_recv, pot_halo_send, pot_halo_recv, in_send, in_recv, halo_send, halo_recv,
+def kernel(psi_hbm, pot, out, psi, snd, own_pot, pots, centre, u0, u1, u2, u3, u4, u5, crossed_z, matrix, outs, back, mixed, gram, *sems):
+    us = (u1, u2, u3, u4, u5)
+    (psi_in, pot_send, pot_recv, pot_halo_send, pot_halo_recv, in_send, in_recv, halo_send, halo_recv,
      gram_send, gram_recv, out_send, out_recv) = sems
     z, y, x, st = (lax.axis_index(name) for name in ("dom_0", "dom_1", "dom_2", "st"))
     me = y * NX + x
@@ -115,6 +117,20 @@
         pl.semaphore_signal(barrier, inc=1, device_id=at(offset)[1], device_id_type=MESH)
     for dz in range(1, NZ):
         pl.semaphore_signal(barrier, inc=1, device_id=(lax.rem(z + dz, NZ), y, x, st), device_id_type=MESH)
+
+    load = pltpu.make_async_copy(psi_hbm, psi, psi_in)
+    load.start()
+
+    from_lane = lax.broadcasted_iota(jnp.int32, (128, 128), 0)
+    to_lane = lax.broadcasted_iota(jnp.int32, (128, 128), 1)
+    apart = (from_lane - to_lane) & 63
+    together = (from_lane & 64) == (to_lane & 64)
+    along_z = jnp.where((apart == 1) | (apart == 63), 16.0, jnp.where((apart == 2) | (apart == 62), -1.0, 0.0))
+    along_z = jnp.where(together, along_z, 0.0)
+    swapped = jnp.where((from_lane ^ 64) == to_lane, 1.0, 0.0)
+    for piece in range(2):
+        matrix[128 * piece : 128 * piece + 128, 0:128] = along_z.astype(jnp.bfloat16)
+        matrix[128 * piece : 128 * piece + 128, 128:256] = swapped.astype(jnp.bfloat16)
 
     for j in range(2):
         tile = jnp.concatenate([pot[0:4, j, :], pot[4:8, j, :]], axis=1)
@@ -144,6 +160,7 @@
                 device_id=where, device_id_type=MESH,
             ).start()
 
+    load.wait()
     to_peers(0)
     pl.semaphore_wait(barrier, len(OFFSETS) + NZ - 1)
     for number, offset in enumerate(OFFSETS):
@@ -244,46 +261,45 @@
 
     low_mask = jnp.where(has_low, 1.0, 0.0)
     high_mask = jnp.where(has_high, 1.0, 0.0)
-    half = lane & 64
-    spot = lane & 63
-    shifts = [half | ((spot + d) & 63) for d in (-1, 1, -2, 2)]
-
-    def pick(value, index):
-        return jnp.take_along_axis(value, index, axis=1, mode="promise_in_bounds")
-
-    centre = (3.75 - SHIFT) * (2.0 / RADIUS)
-    near_w = -(2.0 / 3.0) * (2.0 / RADIUS)
+    centre[...] = (2.0 / RADIUS) * pots[...] + (3.75 - SHIFT) * (2.0 / RADIUS)
     far_w = (1.0 / 24.0) * (2.0 / RADIUS)
 
+    def source(k):
+        return us[k - 1] if k else u0
+
+    def cross(chunk, k, first, count):
+        value = source(k)[chunk, first : first + count].reshape(count * 64, 128)
+        top = value.astype(jnp.bfloat16)
+        rest = (value - top.astype(jnp.float32)).astype(jnp.bfloat16)
+        crossed_z[first * 64 : (first + count) * 64, :] = jnp.dot(
+            jnp.concatenate([top, rest], axis=1), matrix[...], preferred_element_type=jnp.float32
+        )
+
     def apply(chunk, k, b, mask):
-        size = 0.5 if k == 0 else 1.0
-        source = (lambda s, j, i: u0[chunk, s, j, i]) if k == 0 else (lambda s, j, i: us[chunk, k - 1, s, j, i])
-        before = [[source(b - 1, j, i) for i in range(4)] for j in range(2)]
-        here = [[source(b, j, i) for i in range(4)] for j in range(2)]
-        after = [[source(b + 1, j, i) for i in range(4)] for j in range(2)]
-        rows = [before[0], before[1], here[0], here[1], after[0], after[1]]
+        u = source(k)
+        rows = [[u[chunk, b + s, j, i] for i in range(4)] for s in (-1, 0, 1) for j in range(2)]
         values, results = [], []
         for j in range(2):
             row = rows[2 + j]
-            swap = [pltpu.roll(v, 64, 1) for v in row]
+            start = b * 64 + j * 32
+            swap = [crossed_z[start + 8 * i : start + 8 * i + 8, 128:256] for i in range(4)]
             ring = [swap[2], swap[3]] + row + [swap[0], swap[1]]
             for i in range(4):
                 v = row[i]
-                zs = [pick(v, index) for index in shifts]
-                near = (ring[i + 1] + ring[i + 3]) + (rows[1 + j][i] + rows[3 + j][i]) + (zs[0] + zs[1])
-                far = (ring[i] + ring[i + 4]) + (rows[j][i] + rows[4 + j][i]) + (zs[2] + zs[3])
-                weight = (2.0 / RADIUS * size) * pots[b, pl.ds(4 * j + i, 1), :] + centre * size
-                new = weight * v + ((near_w * size) * near + (far_w * size) * far)
-                if k == 1:
-                    new = new - u0[chunk, b, j, i]
-                elif k > 1:
-                    new = new - us[chunk, k - 2, b, j, i]
+                near = (ring[i + 1] + ring[i + 3]) + (rows[1 + j][i] + rows[3 + j][i])
+                far = (ring[i] + ring[i + 4]) + (rows[j][i] + rows[4 + j][i])
+                total = (16.0 * near - far) + crossed_z[start + 8 * i : start + 8 * i + 8, 0:128]
+                new = centre[b, pl.ds(4 * j + i, 1), :] * v - far_w * total
+                if k == 0:
+                    new = 0.5 * new
+                else:
+                    new = new - source(k - 1)[chunk, b, j, i]
                 if mask is not None:
                     new = new * mask
                 values.append(v)
                 results.append(new)
                 if k + 1 < ITERS:
-                    us[chunk, k, b, j, i] = new
+                    us[k][chunk, b, j, i] = new
         return values, results
 
     def tree(values):
@@ -298,24 +314,21 @@
     def moments_of(chunk):
         pairs = []
         for k in range(ITERS):
-            def low_body(b, carry):
-                apply(chunk, k, b, low_mask)
-                return carry
-
-            def high_body(b, carry):
-                apply(chunk, k, b, high_mask)
-                return carry
-
-            def own_body(b, carry):
-                values, results = apply(chunk, k, b, None)
-                same = tree([v * v for v in values])
-                next_ = tree([v * r for v, r in zip(values, results)])
-                return carry[0] + same, carry[1] + next_
-
-            if k + 1 < ITERS:
-                lax.fori_loop(1 + k, HALO, low_body, 0)
-                lax.fori_loop(HALO + PLANE, SLABS - 1 - k, high_body, 0)
-            pairs.append(lax.fori_loop(HALO, HALO + PLANE, own_body, (zero, zero)))
+            first, last = 1 + k, SLABS - 1 - k
+            groups = [(at_, min(GROUP, last - at_)) for at_ in range(first, last, GROUP)]
+            same, next_ = zero, zero
+            cross(chunk, k, *groups[0])
+            for number, (start, count) in enumerate(groups):
+                if number + 1 < len(groups):
+                    cross(chunk, k, *groups[number + 1])
+                for b in range(start, start + count):
+                    mine = HALO <= b < HALO + PLANE
+                    mask = None if mine else (low_mask if b < HALO else high_mask)
+                    values, results = apply(chunk, k, b, mask)
+                    if mine:
+                        same = same + tree([v * v for v in values])
+                        next_ = next_ + tree([v * r for v, r in zip(values, results)])
+            pairs.append((same, next_))
         tile = zero
         for k, pair in enumerate(pairs):
             for odd in range(2):
@@ -331,7 +344,7 @@
                 device_id=(lax.rem(z + dz, NZ), y, x, st), device_id_type=MESH,
             ).start()
 
-    for chunk in range(CHUNKS):
+    def advance(chunk, carry):
         for slot in range(HALO):
             @pl.when(has_low)
             def _():
@@ -342,6 +355,9 @@
                 halo_copy(chunk, slot, False).wait_recv()
         gram[chunk, z] = moments_of(chunk)
         send_gram(chunk)
+        return carry
+
+    lax.fori_loop(0, CHUNKS, advance, 0)
 
     def finish(chunk):
         for p in range(NZ):
@@ -361,7 +377,7 @@
                     v = u0[chunk, HALO + q, j, i]
                     straight, crossed = real[0] * v, imag[0] * v
                     for k in range(1, ITERS):
-                        v = us[chunk, k - 1, HALO + q, j, i]
+                        v = us[k - 1][chunk, HALO + q, j, i]
                         straight = straight + real[k] * v
                         crossed = crossed + imag[k] * v
                     outs[chunk, q, j, i] = straight + pltpu.roll(crossed, 4, 0)
@@ -431,26 +447,29 @@
     result = pl.pallas_call(
         kernel,
         out_shape=jax.ShapeDtypeStruct((parts, cx, by, nz, orbs), jnp.float32),
-        in_specs=[pl.BlockSpec(memory_space=pltpu.VMEM)] * 2,
+        in_specs=[pl.BlockSpec(memory_space=pl.ANY), pl.BlockSpec(memory_space=pltpu.VMEM)],
         out_specs=pl.BlockSpec(memory_space=pltpu.VMEM),
         scratch_shapes=[
+            pltpu.VMEM((parts, cx, by, nz, orbs), jnp.float32),
             pltpu.VMEM((CHUNKS, PLANE) + tiles, jnp.float32),
             pltpu.VMEM((8, 128), jnp.float32),
             pltpu.VMEM((SLABS, 8, 128), jnp.float32),
-            pltpu.VMEM((CHUNKS, SLABS) + tiles, jnp.float32),
-            pltpu.VMEM((CHUNKS, ITERS - 1, SLABS) + tiles, jnp.float32),
+            pltpu.VMEM((SLABS, 8, 128), jnp.float32),
+            *[pltpu.VMEM((CHUNKS, SLABS) + tiles, jnp.float32)] * ITERS,
+            pltpu.VMEM((SLABS * 64, 256), jnp.float32),
+            pltpu.VMEM((256, 256), jnp.bfloat16),
             pltpu.VMEM((CHUNKS, PLANE) + tiles, jnp.float32),
             pltpu.VMEM((CHUNKS, PLANE) + tiles, jnp.float32),
             pltpu.VMEM((2, 4, 128, 128), jnp.float32),
             pltpu.VMEM((CHUNKS, NZ, 8, 128), jnp.float32),
-            dma((peers,)), dma((PLANE,)), dma((2,)), dma((2,)),
+            dma, dma((peers,)), dma((PLANE,)), dma((2,)), dma((2,)),
             dma((CHUNKS, peers)), dma((CHUNKS, PLANE)),
             dma((CHUNKS, 2, HALO)), dma((CHUNKS, 2, HALO)),
             dma((CHUNKS, NZ)), dma((CHUNKS, NZ)),
             dma((CHUNKS, peers)), dma((CHUNKS, PLANE)),
         ],
         compiler_params=pltpu.CompilerParams(
-            collective_id=0, has_side_effects=True, vmem_limit_bytes=48 * 1024 * 1024
+            collective_id=0, has_side_effects=True, vmem_limit_bytes=67043328
         ),
     )(psi.reshape(parts, cx, by, nz, orbs), potential.reshape(cx, by, nz))
     return result.reshape(psi.shape)

time: 88.7 us -> 54.2 us (0.61)
  Pallas kernels: 85.7 us -> 51.7 us
    pallas_call x1, Pallas kernels: 85.7 us -> 51.7 us  [on_device(): pl.pallas_call(kernel, out_shape=jax.ShapeDtypeStruct((parts, cx, by, nz,...]
    unnamed x5 -> x1, local copies, waits for them, and re-layouts: 2.89 us -> 2.31 us
where the time goes in v2:
time: 54.2 us; the launch traced here: 54 us
  Pallas kernels  51.7 us (95%)
  local copies, waits for them, and re-layouts  2.31 us (4%)
    pallas_call x1, Pallas kernels, on_device(): pl.pallas_call(kernel, out_shape=jax.ShapeDtypeStruct((parts, cx, by, nz,...  51.7 us
    unnamed x1, local copies, waits for them, and re-layouts  2.31 us

profile of v2, /device:TPU:8, one launch (start us, length us, event | category | flops | bytes accessed | tf_op | source)
XLA Modules:
  0.0 54.0 jit_solution(17048156490161760353)
XLA Ops:
  0.0 51.7 %shard_map.28 = f32[2,8,2,64,128]{4,3,2,1,0:T(8,128)} custom-call(f32[2,8,2,64,128]{4,3,2,1,0:T(8,128)} %bitcast.6, f32[8,2,64]{2,1,0:T(2,128)} %bitcast.7), custom_call_target="tpu_custom_call" | custom-call | tf_op jit(solution)/shard_map/pallas_call | solution.py:447
  51.7 2.3 %copy.5 = f32[2,1,8,2,64,128]{5,4,3,2,1,0:T(8,128)} copy(f32[2,1,8,2,64,128]{5,4,3,2,1,0:T(8,128)} %bitcast.5) | data formatting | bytes 2097152

commit v3 on v2

--- a/solution.py
+++ b/solution.py
@@ -98,9 +98,9 @@
     return weights
 
 
-def kernel(psi_hbm, pot, out, psi, snd, own_pot, pots, centre, u0, u1, u2, u3, u4, u5, crossed_z, matrix, outs, back, mixed, gram, *sems):
+def kernel(psi_hbm, pot_hbm, out, psi, pot, snd, own_pot, pots, centre, u0, u1, u2, u3, u4, u5, crossed_z, matrix, partial, outs, back, mixed, gram, *sems):
     us = (u1, u2, u3, u4, u5)
-    (psi_in, pot_send, pot_recv, pot_halo_send, pot_halo_recv, in_send, in_recv, halo_send, halo_recv,
+    (psi_in, pot_in, pot_send, pot_recv, pot_halo_send, pot_halo_recv, in_send, in_recv, halo_send, halo_recv,
      gram_send, gram_recv, out_send, out_recv) = sems
     z, y, x, st = (lax.axis_index(name) for name in ("dom_0", "dom_1", "dom_2", "st"))
     me = y * NX + x
@@ -120,6 +120,8 @@
 
     load = pltpu.make_async_copy(psi_hbm, psi, psi_in)
     load.start()
+    load_pot = pltpu.make_async_copy(pot_hbm, pot, pot_in)
+    load_pot.start()
 
     from_lane = lax.broadcasted_iota(jnp.int32, (128, 128), 0)
     to_lane = lax.broadcasted_iota(jnp.int32, (128, 128), 1)
@@ -132,6 +134,7 @@
         matrix[128 * piece : 128 * piece + 128, 0:128] = along_z.astype(jnp.bfloat16)
         matrix[128 * piece : 128 * piece + 128, 128:256] = swapped.astype(jnp.bfloat16)
 
+    load_pot.wait()
     for j in range(2):
         tile = jnp.concatenate([pot[0:4, j, :], pot[4:8, j, :]], axis=1)
         own_pot[4 * j : 4 * j + 4, :] = tile
@@ -156,7 +159,7 @@
             peer, where = at(offset)
             pltpu.make_async_remote_copy(
                 src_ref=snd.at[chunk, peer], dst_ref=u0.at[chunk, HALO + me],
-                send_sem=in_send.at[chunk, number], recv_sem=in_recv.at[chunk, me],
+                send_sem=in_send.at[chunk], recv_sem=in_recv.at[chunk, me],
                 device_id=where, device_id_type=MESH,
             ).start()
 
@@ -167,7 +170,7 @@
         peer, where = at(offset)
         pltpu.make_async_remote_copy(
             src_ref=own_pot, dst_ref=pots.at[HALO + me],
-            send_sem=pot_send.at[number], recv_sem=pot_recv.at[me],
+            send_sem=pot_send, recv_sem=pot_recv,
             device_id=where, device_id_type=MESH,
         ).start()
     send_in(0)
@@ -208,7 +211,7 @@
         target = slot if up else HALO + PLANE + slot
         return pltpu.make_async_remote_copy(
             src_ref=u0.at[chunk, source], dst_ref=u0.at[chunk, target],
-            send_sem=halo_send.at[chunk, int(up), slot], recv_sem=halo_recv.at[chunk, int(up), slot],
+            send_sem=halo_send.at[chunk, int(up)], recv_sem=halo_recv.at[chunk, int(up)],
             device_id=above if up else below, device_id_type=MESH,
         )
 
@@ -235,10 +238,7 @@
                 def _():
                     halo_copy(chunk, p - PLANE + HALO, True).start()
 
-    for p in range(PLANE):
-        @pl.when(me != p)
-        def _():
-            wait_recv(pots.at[HALO + p], pot_recv.at[p])
+    wait_recv(pots.at[pl.ds(0, PLANE - 1)], pot_recv)
 
     @pl.when(has_low)
     def _():
@@ -247,21 +247,15 @@
     @pl.when(has_high)
     def _():
         pot_halo_copy(True).start()
-
-    for chunk in range(CHUNKS):
-        forward(chunk)
-
-    @pl.when(has_low)
-    def _():
-        pot_halo_copy(True).wait_recv()
-
-    @pl.when(has_high)
-    def _():
-        pot_halo_copy(False).wait_recv()
 
     low_mask = jnp.where(has_low, 1.0, 0.0)
     high_mask = jnp.where(has_high, 1.0, 0.0)
-    centre[...] = (2.0 / RADIUS) * pots[...] + (3.75 - SHIFT) * (2.0 / RADIUS)
+
+    def set_centre(first, count):
+        scaled = (2.0 / RADIUS) * pots[first : first + count] + (3.75 - SHIFT) * (2.0 / RADIUS)
+        centre[first : first + count] = scaled
+
+    set_centre(HALO, PLANE)
     far_w = (1.0 / 24.0) * (2.0 / RADIUS)
 
     def source(k):
@@ -311,28 +305,44 @@
 
     zero = jnp.zeros((8, 128), jnp.float32)
 
-    def moments_of(chunk):
-        pairs = []
+    def run(chunk, k, ranges, sums):
+        groups = []
+        for first, last in ranges:
+            groups += [(start, min(GROUP, last - start)) for start in range(first, last, GROUP)]
+        cross(chunk, k, *groups[0])
+        for number, (start, count) in enumerate(groups):
+            if number + 1 < len(groups):
+                cross(chunk, k, *groups[number + 1])
+            for b in range(start, start + count):
+                mine = HALO <= b < HALO + PLANE
+                mask = None if mine else (low_mask if b < HALO else high_mask)
+                values, results = apply(chunk, k, b, mask)
+                if mine:
+                    sums = (
+                        sums[0] + tree([v * v for v in values]),
+                        sums[1] + tree([v * r for v, r in zip(values, results)]),
+                    )
+        return sums
+
+    def inner_range(k):
+        return HALO + 1 + k, HALO + PLANE - 1 - k
+
+    def inner(chunk, carry):
+        forward(chunk)
         for k in range(ITERS):
-            first, last = 1 + k, SLABS - 1 - k
-            groups = [(at_, min(GROUP, last - at_)) for at_ in range(first, last, GROUP)]
-            same, next_ = zero, zero
-            cross(chunk, k, *groups[0])
-            for number, (start, count) in enumerate(groups):
-                if number + 1 < len(groups):
-                    cross(chunk, k, *groups[number + 1])
-                for b in range(start, start + count):
-                    mine = HALO <= b < HALO + PLANE
-                    mask = None if mine else (low_mask if b < HALO else high_mask)
-                    values, results = apply(chunk, k, b, mask)
-                    if mine:
-                        same = same + tree([v * v for v in values])
-                        next_ = next_ + tree([v * r for v, r in zip(values, results)])
-            pairs.append((same, next_))
+            sums = run(chunk, k, [inner_range(k)], (zero, zero))
+            for odd in range(2):
+                partial[chunk, 2 * k + odd] = sums[odd]
+        return carry
+
+    def outer(chunk):
         tile = zero
-        for k, pair in enumerate(pairs):
+        for k in range(ITERS):
+            first, last = inner_range(k)
+            sums = (partial[chunk, 2 * k], partial[chunk, 2 * k + 1])
+            sums = run(chunk, k, [(1 + k, first), (last, SLABS - 1 - k)], sums)
             for odd in range(2):
-                total = jnp.sum(pair[odd], axis=1, keepdims=True)
+                total = jnp.sum(sums[odd], axis=1, keepdims=True)
                 tile = jnp.where(lane == 2 * k + odd, total, tile)
         return tile
 
@@ -340,30 +350,54 @@
         for dz in range(1, NZ):
             pltpu.make_async_remote_copy(
                 src_ref=gram.at[chunk, z], dst_ref=gram.at[chunk, z],
-                send_sem=gram_send.at[chunk, dz], recv_sem=gram_recv.at[chunk, z],
+                send_sem=gram_send.at[chunk], recv_sem=gram_recv.at[chunk],
                 device_id=(lax.rem(z + dz, NZ), y, x, st), device_id_type=MESH,
             ).start()
 
     def advance(chunk, carry):
-        for slot in range(HALO):
-            @pl.when(has_low)
-            def _():
-                halo_copy(chunk, slot, True).wait_recv()
-
-            @pl.when(has_high)
-            def _():
-                halo_copy(chunk, slot, False).wait_recv()
-        gram[chunk, z] = moments_of(chunk)
+        @pl.when(has_low)
+        def _():
+            wait_recv(u0.at[chunk, pl.ds(0, HALO)], halo_recv.at[chunk, 1])
+
+        @pl.when(has_high)
+        def _():
+            wait_recv(u0.at[chunk, pl.ds(0, HALO)], halo_recv.at[chunk, 0])
+        gram[chunk, z] = outer(chunk)
         send_gram(chunk)
         return carry
 
+    lax.fori_loop(0, CHUNKS, inner, 0)
+
+    @pl.when(has_low)
+    def _():
+        pot_halo_copy(True).wait_recv()
+
+    @pl.when(has_high)
+    def _():
+        pot_halo_copy(False).wait_recv()
+
+    set_centre(0, HALO)
+    set_centre(HALO + PLANE, HALO)
     lax.fori_loop(0, CHUNKS, advance, 0)
 
+    wait_send(pots.at[pl.ds(0, PLANE - 1)], pot_send)
+    for chunk in range(CHUNKS):
+        wait_send(snd.at[chunk, pl.ds(0, PLANE - 1)], in_send.at[chunk])
+
+    @pl.when(has_low)
+    def _():
+        pot_halo_copy(False).wait_send()
+        for chunk in range(CHUNKS):
+            wait_send(u0.at[chunk, pl.ds(0, HALO)], halo_send.at[chunk, 0])
+
+    @pl.when(has_high)
+    def _():
+        pot_halo_copy(True).wait_send()
+        for chunk in range(CHUNKS):
+            wait_send(u0.at[chunk, pl.ds(0, HALO)], halo_send.at[chunk, 1])
+
     def finish(chunk):
-        for p in range(NZ):
-            @pl.when(z != p)
-            def _():
-                wait_recv(gram.at[chunk, p], gram_recv.at[chunk, p])
+        wait_recv(gram.at[chunk, pl.ds(0, NZ - 1)], gram_recv.at[chunk])
         total = tree([gram[chunk, p] for p in range(NZ)])
         total = total + pltpu.roll(total, 4, 0)
         raw = [jnp.broadcast_to(total[:, l : l + 1], (8, 128)) for l in range(2 * ITERS)]
@@ -371,7 +405,7 @@
         real, imag = lanczos_weights(moments)
         imag = [jnp.where(sub < 4, value, -value) for value in imag]
 
-        def combine(q, carry):
+        def combine(q, put):
             for j in range(2):
                 for i in range(4):
                     v = u0[chunk, HALO + q, j, i]
@@ -380,27 +414,37 @@
                         v = us[k - 1][chunk, HALO + q, j, i]
                         straight = straight + real[k] * v
                         crossed = crossed + imag[k] * v
-                    outs[chunk, q, j, i] = straight + pltpu.roll(crossed, 4, 0)
-            return carry
-
-        lax.fori_loop(0, PLANE, combine, 0)
-        for number, offset in enumerate(OFFSETS):
+                    put(j, i, straight + pltpu.roll(crossed, 4, 0))
+
+        def send_out(offset):
             peer, where = at(offset)
             pltpu.make_async_remote_copy(
                 src_ref=outs.at[chunk, peer], dst_ref=back.at[chunk, me],
-                send_sem=out_send.at[chunk, number], recv_sem=out_recv.at[chunk, me],
+                send_sem=out_send.at[chunk], recv_sem=out_recv.at[chunk],
                 device_id=where, device_id_type=MESH,
             ).start()
-        back[chunk, me] = outs[chunk, me]
+
+        for number, offset in enumerate(OFFSETS):
+            peer = at(offset)[0]
+
+            def put(j, i, value):
+                outs[chunk, peer, j, i] = value
+
+            combine(peer, put)
+            if number:
+                send_out(OFFSETS[number - 1])
+
+        def keep(j, i, value):
+            back[chunk, me, j, i] = value
+
+        combine(me, keep)
+        send_out(OFFSETS[-1])
 
     for chunk in range(CHUNKS):
         finish(chunk)
 
     for chunk in range(CHUNKS):
-        for p in range(PLANE):
-            @pl.when(me != p)
-            def _():
-                wait_recv(back.at[chunk, p], out_recv.at[chunk, p])
+        wait_recv(back.at[chunk, pl.ds(0, PLANE - 1)], out_recv.at[chunk])
         for j in range(2):
             for i in range(4):
                 cells = back[chunk, :, j, i].reshape(128, 128).T
@@ -415,42 +459,23 @@
                     out[1, i, j] = im[0:64]
                     out[1, i + 4, j] = im[64:128]
 
-    for number in range(len(OFFSETS)):
-        wait_send(own_pot, pot_send.at[number])
-        for chunk in range(CHUNKS):
-            wait_send(snd.at[chunk, 0], in_send.at[chunk, number])
-            wait_send(outs.at[chunk, 0], out_send.at[chunk, number])
     for chunk in range(CHUNKS):
-        for dz in range(1, NZ):
-            wait_send(gram.at[chunk, 0], gram_send.at[chunk, dz])
-
-    @pl.when(has_low)
-    def _():
-        pot_halo_copy(False).wait_send()
-        for chunk in range(CHUNKS):
-            for slot in range(HALO):
-                halo_copy(chunk, slot, False).wait_send()
-
-    @pl.when(has_high)
-    def _():
-        pot_halo_copy(True).wait_send()
-        for chunk in range(CHUNKS):
-            for slot in range(HALO):
-                halo_copy(chunk, slot, True).wait_send()
+        wait_send(gram.at[chunk, pl.ds(0, NZ - 1)], gram_send.at[chunk])
+        wait_send(outs.at[chunk, pl.ds(0, PLANE - 1)], out_send.at[chunk])
 
 
 def on_device(psi, potential):
     parts, _, cx, by, nz, orbs = psi.shape
     dma = pltpu.SemaphoreType.DMA
-    peers = len(OFFSETS)
     tiles = (2, 4, 8, 128)
     result = pl.pallas_call(
         kernel,
         out_shape=jax.ShapeDtypeStruct((parts, cx, by, nz, orbs), jnp.float32),
-        in_specs=[pl.BlockSpec(memory_space=pl.ANY), pl.BlockSpec(memory_space=pltpu.VMEM)],
+        in_specs=[pl.BlockSpec(memory_space=pltpu.HBM)] * 2,
         out_specs=pl.BlockSpec(memory_space=pltpu.VMEM),
         scratch_shapes=[
             pltpu.VMEM((parts, cx, by, nz, orbs), jnp.float32),
+            pltpu.VMEM((cx, by, nz), jnp.float32),
             pltpu.VMEM((CHUNKS, PLANE) + tiles, jnp.float32),
             pltpu.VMEM((8, 128), jnp.float32),
             pltpu.VMEM((SLABS, 8, 128), jnp.float32),
@@ -458,18 +483,19 @@
             *[pltpu.VMEM((CHUNKS, SLABS) + tiles, jnp.float32)] * ITERS,
             pltpu.VMEM((SLABS * 64, 256), jnp.float32),
             pltpu.VMEM((256, 256), jnp.bfloat16),
+            pltpu.VMEM((CHUNKS, 2 * ITERS, 8, 128), jnp.float32),
             pltpu.VMEM((CHUNKS, PLANE) + tiles, jnp.float32),
             pltpu.VMEM((CHUNKS, PLANE) + tiles, jnp.float32),
             pltpu.VMEM((2, 4, 128, 128), jnp.float32),
             pltpu.VMEM((CHUNKS, NZ, 8, 128), jnp.float32),
-            dma, dma((peers,)), dma((PLANE,)), dma((2,)), dma((2,)),
-            dma((CHUNKS, peers)), dma((CHUNKS, PLANE)),
-            dma((CHUNKS, 2, HALO)), dma((CHUNKS, 2, HALO)),
-            dma((CHUNKS, NZ)), dma((CHUNKS, NZ)),
-            dma((CHUNKS, peers)), dma((CHUNKS, PLANE)),
+            dma, dma, dma, dma, dma((2,)), dma((2,)),
+            dma((CHUNKS,)), dma((CHUNKS, PLANE)),
+            dma((CHUNKS, 2)), dma((CHUNKS, 2)),
+            dma((CHUNKS,)), dma((CHUNKS,)),
+            dma((CHUNKS,)), dma((CHUNKS,)),
         ],
         compiler_params=pltpu.CompilerParams(
-            collective_id=0, has_side_effects=True, vmem_limit_bytes=67043328
+            collective_id=0, has_side_effects=True, vmem_limit_bytes=48000000
         ),
     )(psi.reshape(parts, cx, by, nz, orbs), potential.reshape(cx, by, nz))
     return result.reshape(psi.shape)

time: 54.2 us -> 49.6 us (0.915)
  Pallas kernels: 51.7 us -> 46.4 us
  local copies, waits for them, and re-layouts: 2.31 us -> 2.89 us
    pallas_call x1, Pallas kernels: 51.7 us -> 46.4 us  [on_device(): pl.pallas_call(kernel, out_shape=jax.ShapeDtypeStruct((parts, cx, by, nz,...]
    unnamed x1 -> x5, local copies, waits for them, and re-layouts: 2.31 us -> 2.89 us
where the time goes in v3:
time: 49.6 us; the launch traced here: 49.3 us
  Pallas kernels  46.4 us (94%)
  local copies, waits for them, and re-layouts  2.89 us (6%)
    pallas_call x1, Pallas kernels, on_device(): pl.pallas_call(kernel, out_shape=jax.ShapeDtypeStruct((parts, cx, by, nz,...  46.4 us
    unnamed x5, local copies, waits for them, and re-layouts  2.89 us

profile of v3, /device:TPU:8, one launch (start us, length us, event | category | flops | bytes accessed | tf_op | source)
XLA Modules:
  0.0 49.3 jit_solution(14989598975026404036)
XLA Ops:
  0.0 0.0 copy-start
  0.0 1.2 %copy-done = f32[2,1,8,2,64,128]{5,4,3,2,1,0:T(8,128)S(1)} copy-done((f32[2,1,8,2,64,128]{5,4,3,2,1,0:T(8,128)S(1)}, f32[2,1,8,2,64,128]{5,4,3,2,1,0:T(8,128)}, u32[]{:S(2)}) %copy-start) | copy-done | bytes 1048600
  1.2 0.0 copy-start.1
  1.2 0.7 %copy-done.1 = f32[1,8,2,64]{3,2,1,0:T(2,128)S(1)} copy-done((f32[1,8,2,64]{3,2,1,0:T(2,128)S(1)}, f32[1,8,2,64]{3,2,1,0:T(2,128)}, u32[]{:S(2)}) %copy-start.1) | copy-done | bytes 4120
  1.9 46.4 %shard_map.28 = f32[2,8,2,64,128]{4,3,2,1,0:T(8,128)S(1)} custom-call(f32[2,8,2,64,128]{4,3,2,1,0:T(8,128)S(1)} %bitcast.6, f32[8,2,64]{2,1,0:T(2,128)S(1)} %bitcast.7), custom_call_target="tpu_custom_call" | custom-call | tf_op jit(solution)/shard_map/pallas_call | solution.py:471
  48.3 1.0 %copy.5 = f32[2,1,8,2,64,128]{5,4,3,2,1,0:T(8,128)} copy(f32[2,1,8,2,64,128]{5,4,3,2,1,0:T(8,128)S(1)} %bitcast.5) | data formatting | bytes 2097152
Async XLA Ops:
  0.0 1.2 %copy-start = (f32[2,1,8,2,64,128]{5,4,3,2,1,0:T(8,128)S(1)}, f32[2,1,8,2,64,128]{5,4,3,2,1,0:T(8,128)}, u32[]{:S(2)}) copy-start(f32[2,1,8,2,64,128]{5,4,3,2,1,0:T(8,128)} %param.2) | copy-start | bytes 3145732
  1.2 0.7 %copy-start.1 = (f32[1,8,2,64]{3,2,1,0:T(2,128)S(1)}, f32[1,8,2,64]{3,2,1,0:T(2,128)}, u32[]{:S(2)}) copy-start(f32[1,8,2,64]{3,2,1,0:T(2,128)} %param.3) | copy-start | bytes 12292

commit v4 on v3

v4 whole, which is shorter than its diff:
```python
import jax
import jax.numpy as jnp
from jax import lax
from jax.experimental import pallas as pl
from jax.experimental.pallas import tpu as pltpu
from jax.sharding import Mesh
from jax.sharding import PartitionSpec as P

MESH = pl.DeviceIdType.MESH
ITERS = 6
TERMS = 32
EPS = 1e-6
STEP = 0.5
SHIFT = 6.0
RADIUS = 6.0
HALO = 6
NX, NY, NZ = 4, 4, 8
PLANE = NX * NY
SLABS = PLANE + 2 * HALO
CHUNKS = 4
ORBS = 2
GROUP = 8
OFFSETS = (
    (2, 2), (2, 1), (1, 2), (2, 3), (3, 2), (1, 1), (3, 3), (1, 3), (3, 1),
    (2, 0), (0, 2), (1, 0), (0, 1), (3, 0), (0, 3),
)


def lanczos_weights(moments):
    first_norm = jnp.sqrt(moments[0] + EPS)
    inverse = 1.0 / first_norm
    sig = [value * inverse for value in moments]
    coef = [inverse]
    sig_prev, coef_prev, beta_prev = None, None, None
    alphas, betas, basis = [], [], []
    for j in range(ITERS):
        count = 2 * ITERS - 1 - j
        shifted = [0.5 * RADIUS * (sig[l + 1] + sig[abs(l - 1)]) for l in range(count)]
        alpha = coef[0] * (SHIFT * sig[0] + shifted[0])
        for k in range(1, j + 1):
            alpha = alpha + coef[k] * (SHIFT * sig[k] + shifted[k])
        alpha = jnp.clip(alpha, 0.0, 12.0)
        alphas.append(alpha)
        basis.append(coef)
        if j + 1 == ITERS:
            break
        rest = SHIFT - alpha
        r_sig = [shifted[l] + rest * sig[l] for l in range(count)]
        if j:
            r_sig = [r_sig[l] - beta_prev * sig_prev[l] for l in range(count)]
        r_coef = []
        for k in range(j + 2):
            terms = []
            if k >= 1:
                terms.append((RADIUS if k == 1 else 0.5 * RADIUS) * coef[k - 1])
            if k + 1 <= j:
                terms.append(0.5 * RADIUS * coef[k + 1])
            if k <= j:
                terms.append(rest * coef[k])
            if j and k < j:
                terms.append(-(beta_prev * coef_prev[k]))
            total = terms[0]
            for term in terms[1:]:
                total = total + term
            r_coef.append(total)
        square = r_coef[0] * r_sig[0]
        for k in range(1, j + 2):
            square = square + r_coef[k] * r_sig[k]
        beta = jnp.sqrt(jnp.clip(square, 0.0, 36.5) + EPS)
        betas.append(beta)
        scale = 1.0 / beta
        sig_prev, coef_prev, beta_prev = sig, coef, beta
        sig = [jnp.clip(value * scale, -first_norm, first_norm) for value in r_sig]
        coef = [value * scale for value in r_coef]
    zero = jnp.zeros_like(first_norm)
    term = [zero + 1.0] + [zero] * (ITERS - 1)
    sums = [list(term), [zero] * ITERS]
    for order in range(1, TERMS):
        factor = STEP / order if order % 2 == 0 else -STEP / order
        applied = []
        for i in range(ITERS):
            value = alphas[i] * term[i]
            if i + 1 < ITERS:
                value = value + betas[i] * term[i + 1]
            if i:
                value = value + betas[i - 1] * term[i - 1]
            applied.append(factor * value)
        term = applied
        sums[order % 2] = [a + b for a, b in zip(sums[order % 2], term)]
    weights = []
    for part in range(2):
        row = []
        for k in range(ITERS):
            total = sums[part][k] * basis[k][k]
            for j in range(k + 1, ITERS):
                total = total + sums[part][j] * basis[j][k]
            row.append(first_norm * total)
        weights.append(row)
    return weights


def kernel(psi_hbm, pot_hbm, out, psi, pot, snd, own_pot, pots, centre, u0, u1, u2, u3, u4, u5, crossed_z, matrix, partial, outs, back, mixed, gram, *sems):
    us = (u1, u2, u3, u4, u5)
    (psi_in, pot_in, pot_send, pot_recv, pot_halo_send, pot_halo_recv, in_send, in_recv, halo_send, halo_recv,
     gram_send, gram_recv, out_send, out_recv) = sems
    z, y, x, st = (lax.axis_index(name) for name in ("dom_0", "dom_1", "dom_2", "st"))
    me = y * NX + x
    lane = lax.broadcasted_iota(jnp.int32, (8, 128), 1)
    sub = lax.broadcasted_iota(jnp.int32, (8, 128), 0)

    def at(offset):
        to_y = lax.rem(y + offset[0], NY)
        to_x = lax.rem(x + offset[1], NX)
        return to_y * NX + to_x, (z, to_y, to_x, st)

    barrier = pltpu.get_barrier_semaphore()
    for offset in OFFSETS:
        pl.semaphore_signal(barrier, inc=1, device_id=at(offset)[1], device_id_type=MESH)
    for dz in range(1, NZ):
        pl.semaphore_signal(barrier, inc=1, device_id=(lax.rem(z + dz, NZ), y, x, st), device_id_type=MESH)

    load = pltpu.make_async_copy(psi_hbm, psi, psi_in)
    load.start()
    load_pot = pltpu.make_async_copy(pot_hbm, pot, pot_in)
    load_pot.start()

    from_lane = lax.broadcasted_iota(jnp.int32, (128, 128), 0)
    to_lane = lax.broadcasted_iota(jnp.int32, (128, 128), 1)
    apart = (from_lane - to_lane) & 63
    together = (from_lane & 64) == (to_lane & 64)
    along_z = jnp.where((apart == 1) | (apart == 63), 16.0, jnp.where((apart == 2) | (apart == 62), -1.0, 0.0))
    along_z = jnp.where(together, along_z, 0.0)
    swapped = jnp.where((from_lane ^ 64) == to_lane, 1.0, 0.0)
    for piece in range(2):
        matrix[128 * piece : 128 * piece + 128, 0:128] = along_z.astype(jnp.bfloat16)
        matrix[128 * piece : 128 * piece + 128, 128:256] = swapped.astype(jnp.bfloat16)

    load_pot.wait()
    for j in range(2):
        tile = jnp.concatenate([pot[0:4, j, :], pot[4:8, j, :]], axis=1)
        own_pot[4 * j : 4 * j + 4, :] = tile
    pots[HALO + me] = own_pot[...]

    wide = lax.broadcasted_iota(jnp.int32, (128, 128), 1)
    group = lax.shift_right_logical(wide, 1) & 3

    def merged(tiles, number):
        total = None
        for g in range(4):
            moved = tiles[g] if g == number else pltpu.roll(tiles[g], (2 * (g - number)) % 128, 1)
            total = moved if total is None else jnp.where(group == g, moved, total)
        return total

    def to_peers(chunks):
        for i in range(4):
            tiles = [
                jnp.concatenate([psi[part, i, j], psi[part, i + 4, j]], axis=0) for j in range(2) for part in range(2)
            ]
            for chunk in chunks:
                snd[chunk, :, i] = merged(tiles, chunk).T.reshape(PLANE, 8, 128)

    def rows(slab, count=1):
        return pl.ds(pl.multiple_of(8 * slab, 8), 8 * count)

    def send_in(chunk):
        for number, offset in enumerate(OFFSETS):
            peer, where = at(offset)
            pltpu.make_async_remote_copy(
                src_ref=snd.at[chunk, peer], dst_ref=u0.at[chunk, :, rows(HALO + me)],
                send_sem=in_send.at[chunk], recv_sem=in_recv.at[chunk, me],
                device_id=where, device_id_type=MESH,
            ).start()

    load.wait()
    to_peers((0,))
    pl.semaphore_wait(barrier, len(OFFSETS) + NZ - 1)
    for number, offset in enumerate(OFFSETS):
        peer, where = at(offset)
        pltpu.make_async_remote_copy(
            src_ref=own_pot, dst_ref=pots.at[HALO + me],
            send_sem=pot_send, recv_sem=pot_recv,
            device_id=where, device_id_type=MESH,
        ).start()
    send_in(0)
    for chunk in range(1, CHUNKS):
        to_peers((chunk,))
        send_in(chunk)
    for chunk in range(CHUNKS):
        u0[chunk, :, rows(HALO + me), :] = snd[chunk, me]

    has_low, has_high = z > 0, z < NZ - 1
    below, above = (jnp.maximum(z - 1, 0), y, x, st), (jnp.minimum(z + 1, NZ - 1), y, x, st)

    @pl.when(jnp.logical_not(has_low))
    def _():
        for chunk in range(CHUNKS):
            u0[chunk, :, 0 : 8 * HALO] = jnp.zeros((4, 8 * HALO, 128), jnp.float32)
        pots[0:HALO] = jnp.zeros((HALO, 8, 128), jnp.float32)

    @pl.when(jnp.logical_not(has_high))
    def _():
        for chunk in range(CHUNKS):
            u0[chunk, :, 8 * (HALO + PLANE) : 8 * SLABS] = jnp.zeros((4, 8 * HALO, 128), jnp.float32)
        pots[HALO + PLANE : SLABS] = jnp.zeros((HALO, 8, 128), jnp.float32)

    def wait_recv(ref, sem):
        pltpu.make_async_remote_copy(
            src_ref=ref, dst_ref=ref, send_sem=sem, recv_sem=sem,
            device_id=(z, y, x, st), device_id_type=MESH,
        ).wait_recv()

    def wait_send(ref, sem):
        pltpu.make_async_remote_copy(
            src_ref=ref, dst_ref=ref, send_sem=sem, recv_sem=sem,
            device_id=(z, y, x, st), device_id_type=MESH,
        ).wait_send()

    def halo_copy(chunk, p, up):
        target = p + HALO - PLANE if up else p + HALO + PLANE
        return pltpu.make_async_remote_copy(
            src_ref=u0.at[chunk, :, rows(HALO + p)], dst_ref=u0.at[chunk, :, rows(target)],
            send_sem=halo_send.at[chunk, int(up)], recv_sem=halo_recv.at[chunk, int(up)],
            device_id=above if up else below, device_id_type=MESH,
        )

    def pot_halo_copy(up):
        source = PLANE if up else HALO
        target = 0 if up else HALO + PLANE
        return pltpu.make_async_remote_copy(
            src_ref=pots.at[pl.ds(source, HALO)], dst_ref=pots.at[pl.ds(target, HALO)],
            send_sem=pot_halo_send.at[int(up)], recv_sem=pot_halo_recv.at[int(up)],
            device_id=above if up else below, device_id_type=MESH,
        )

    def pass_on(chunk, p):
        @pl.when(jnp.logical_and(has_low, p < HALO))
        def _():
            halo_copy(chunk, p, False).start()

        @pl.when(jnp.logical_and(has_high, p >= PLANE - HALO))
        def _():
            halo_copy(chunk, p, True).start()

    def forward(chunk):
        pass_on(chunk, me)
        for offset in OFFSETS:
            p = at((NY - offset[0], NX - offset[1]))[0]
            wait_recv(u0.at[chunk, :, rows(HALO)], in_recv.at[chunk, p])
            pass_on(chunk, p)

    wait_recv(pots.at[pl.ds(0, PLANE - 1)], pot_recv)

    @pl.when(has_low)
    def _():
        pot_halo_copy(False).start()

    @pl.when(has_high)
    def _():
        pot_halo_copy(True).start()

    low_mask = jnp.where(has_low, 1.0, 0.0)
    high_mask = jnp.where(has_high, 1.0, 0.0)

    def set_centre(first, count):
        for b in range(first, first + count):
            for i in range(4):
                tile = jnp.where(sub < 4, pots[b, i : i + 1, :], pots[b, 4 + i : 5 + i, :])
                centre[i, 8 * b : 8 * b + 8] = (2.0 / RADIUS) * tile + (3.75 - SHIFT) * (2.0 / RADIUS)

    set_centre(HALO, PLANE)
    far_w = (1.0 / 24.0) * (2.0 / RADIUS)

    def source(k):
        return us[k - 1] if k else u0

    def cross(k, chunk, first, count):
        value = source(k)[chunk, :, 8 * first : 8 * (first + count)].reshape(count * 32, 128)
        top = value.astype(jnp.bfloat16)
        rest = (value - top.astype(jnp.float32)).astype(jnp.bfloat16)
        product = jnp.dot(
            jnp.concatenate([top, rest], axis=1), matrix[...], preferred_element_type=jnp.float32
        )
        crossed_z[chunk % 2, :, 8 * first : 8 * (first + count)] = product.reshape(4, count * 8, 256)

    def apply(chunk, k, b, mask):
        u = source(k)
        here = slice(8 * b, 8 * b + 8)
        row = [u[chunk, i, here] for i in range(4)]
        swap = [crossed_z[chunk % 2, i, here, 128:256] for i in range(4)]
        ring = [swap[2], swap[3]] + row + [swap[0], swap[1]]
        results = []
        for i in range(4):
            y = [u[chunk, i, 8 * b + 4 * d : 8 * b + 4 * d + 8] for d in (-2, -1, 1, 2)]
            near = (ring[i + 1] + ring[i + 3]) + (y[1] + y[2])
            far = (ring[i] + ring[i + 4]) + (y[0] + y[3])
            total = (16.0 * near - far) + crossed_z[chunk % 2, i, here, 0:128]
            new = centre[i, here] * row[i] - far_w * total
            if k == 0:
                new = 0.5 * new
            else:
                new = new - source(k - 1)[chunk, i, here]
            if mask is not None:
                new = new * mask
            results.append(new)
            if k + 1 < ITERS:
                us[k][chunk, i, here] = new
        return row, results

    def tree(values):
        while len(values) > 1:
            values = [values[i] + values[i + 1] for i in range(0, len(values) - 1, 2)] + (
                [values[-1]] if len(values) % 2 else []
            )
        return values[0]

    zero = jnp.zeros((8, 128), jnp.float32)

    def inner_range(k):
        return HALO + 1 + k, HALO + PLANE - 1 - k

    def step(k, jobs):
        groups = []
        for chunk, ranges in jobs:
            for first, last in ranges:
                groups += [(chunk, start, min(GROUP, last - start)) for start in range(first, last, GROUP)]
        sums = {chunk: (zero, zero) for chunk, _ in jobs}
        cross(k, *groups[0])
        for number, (chunk, start, count) in enumerate(groups):
            if number + 1 < len(groups):
                cross(k, *groups[number + 1])
            for b in range(start, start + count):
                mine = HALO <= b < HALO + PLANE
                mask = None if mine else (low_mask if b < HALO else high_mask)
                values, results = apply(chunk, k, b, mask)
                if mine:
                    same, next_ = sums[chunk]
                    sums[chunk] = (
                        same + tree([v * v for v in values]),
                        next_ + tree([v * r for v, r in zip(values, results)]),
                    )
        return sums

    def advance(inner, outer):
        tile = zero
        for k in range(ITERS):
            first, last = inner_range(k)
            jobs = []
            if outer is not None:
                jobs.append((outer, [(1 + k, first), (last, SLABS - 1 - k)]))
            if inner is not None:
                jobs.append((inner, [(first, last)]))
            sums = step(k, jobs)
            for odd in range(2):
                if inner is not None:
                    partial[inner, 2 * k + odd] = sums[inner][odd]
                if outer is not None:
                    total = sums[outer][odd] + partial[outer, 2 * k + odd]
                    total = jnp.sum(total, axis=1, keepdims=True)
                    tile = jnp.where(lane == 2 * k + odd, total, tile)
        return tile

    def send_gram(chunk):
        for dz in range(1, NZ):
            pltpu.make_async_remote_copy(
                src_ref=gram.at[chunk, z], dst_ref=gram.at[chunk, z],
                send_sem=gram_send.at[chunk], recv_sem=gram_recv.at[chunk],
                device_id=(lax.rem(z + dz, NZ), y, x, st), device_id_type=MESH,
            ).start()

    def wait_halo(chunk):
        @pl.when(has_low)
        def _():
            wait_recv(u0.at[chunk, :, rows(0, HALO)], halo_recv.at[chunk, 1])

        @pl.when(has_high)
        def _():
            wait_recv(u0.at[chunk, :, rows(0, HALO)], halo_recv.at[chunk, 0])

    def finish(chunk):
        wait_recv(gram.at[chunk, pl.ds(0, NZ - 1)], gram_recv.at[chunk])
        total = tree([gram[chunk, p] for p in range(NZ)])
        total = total + pltpu.roll(total, 4, 0)
        total = total + pltpu.roll(total, 2, 0)
        raw = [jnp.broadcast_to(total[:, l : l + 1], (8, 128)) for l in range(2 * ITERS)]
        moments = raw[:2] + [2.0 * raw[l] - raw[l % 2] for l in range(2, 2 * ITERS)]
        real, imag = lanczos_weights(moments)
        real_rows = (sub & 2) == 0
        imag = [jnp.where(real_rows, value, -value) for value in imag]

        def combine(q, put):
            for i in range(4):
                v = u0[chunk, i, rows(HALO + q), :]
                straight, crossed = real[0] * v, imag[0] * v
                for k in range(1, ITERS):
                    v = us[k - 1][chunk, i, rows(HALO + q), :]
                    straight = straight + real[k] * v
                    crossed = crossed + imag[k] * v
                put(i, straight + jnp.where(real_rows, pltpu.roll(crossed, 6, 0), pltpu.roll(crossed, 2, 0)))

        def send_out(offset):
            peer, where = at(offset)
            pltpu.make_async_remote_copy(
                src_ref=outs.at[chunk, peer], dst_ref=back.at[chunk, me],
                send_sem=out_send.at[chunk], recv_sem=out_recv.at[chunk],
                device_id=where, device_id_type=MESH,
            ).start()

        for number, offset in enumerate(OFFSETS):
            peer = at(offset)[0]

            def put(i, value):
                outs[chunk, peer, i] = value

            combine(peer, put)
            if number:
                send_out(OFFSETS[number - 1])

        def keep(i, value):
            back[chunk, me, i] = value

        combine(me, keep)
        send_out(OFFSETS[-1])

    forward(0)
    advance(0, None)
    forward(1)

    @pl.when(has_low)
    def _():
        pot_halo_copy(True).wait_recv()

    @pl.when(has_high)
    def _():
        pot_halo_copy(False).wait_recv()

    set_centre(0, HALO)
    set_centre(HALO + PLANE, HALO)
    for chunk in range(CHUNKS):
        if 1 <= chunk < CHUNKS - 1:
            forward(chunk + 1)
        wait_halo(chunk)
        gram[chunk, z] = advance(chunk + 1 if chunk + 1 < CHUNKS else None, chunk)
        send_gram(chunk)
        if chunk == CHUNKS - 2:
            finish(0)
    for chunk in range(1, CHUNKS):
        finish(chunk)

    wait_send(pots.at[pl.ds(0, PLANE - 1)], pot_send)
    for chunk in range(CHUNKS):
        wait_send(snd.at[chunk, pl.ds(0, PLANE - 1)], in_send.at[chunk])
        wait_send(gram.at[chunk, pl.ds(0, NZ - 1)], gram_send.at[chunk])

    @pl.when(has_low)
    def _():
        pot_halo_copy(False).wait_send()
        for chunk in range(CHUNKS):
            wait_send(u0.at[chunk, :, rows(0, HALO)], halo_send.at[chunk, 0])

    @pl.when(has_high)
    def _():
        pot_halo_copy(True).wait_send()
        for chunk in range(CHUNKS):
            wait_send(u0.at[chunk, :, rows(0, HALO)], halo_send.at[chunk, 1])

    for chunk in range(CHUNKS):
        wait_recv(back.at[chunk, pl.ds(0, PLANE - 1)], out_recv.at[chunk])
        for i in range(4):
            tile = back[chunk, :, i].reshape(128, 128).T
            for g in range(4):
                moved = tile if g == chunk else pltpu.roll(tile, (2 * (chunk - g)) % 128, 1)
                whole = moved if chunk == 0 else jnp.where(group == chunk, moved, mixed[i, g])
                if chunk + 1 < CHUNKS:
                    mixed[i, g] = whole
                else:
                    out[g % 2, i, g // 2] = whole[0:64]
                    out[g % 2, i + 4, g // 2] = whole[64:128]
    for chunk in range(CHUNKS):
        wait_send(outs.at[chunk, pl.ds(0, PLANE - 1)], out_send.at[chunk])


def on_device(psi, potential):
    parts, _, cx, by, nz, orbs = psi.shape
    dma = pltpu.SemaphoreType.DMA
    tiles = (4, 8, 128)
    result = pl.pallas_call(
        kernel,
        out_shape=jax.ShapeDtypeStruct((parts, cx, by, nz, orbs), jnp.float32),
        in_specs=[pl.BlockSpec(memory_space=pl.ANY)] * 2,
        out_specs=pl.BlockSpec(memory_space=pltpu.VMEM),
        scratch_shapes=[
            pltpu.VMEM((parts, cx, by, nz, orbs), jnp.float32),
            pltpu.VMEM((cx, by, nz), jnp.float32),
            pltpu.VMEM((CHUNKS, PLANE) + tiles, jnp.float32),
            pltpu.VMEM((8, 128), jnp.float32),
            pltpu.VMEM((SLABS, 8, 128), jnp.float32),
            pltpu.VMEM((4, 8 * SLABS, 128), jnp.float32),
            *[pltpu.VMEM((CHUNKS, 4, 8 * SLABS, 128), jnp.float32)] * ITERS,
            pltpu.VMEM((2, 4, 8 * SLABS, 256), jnp.float32),
            pltpu.VMEM((256, 256), jnp.bfloat16),
            pltpu.VMEM((CHUNKS, 2 * ITERS, 8, 128), jnp.float32),
            pltpu.VMEM((CHUNKS, PLANE) + tiles, jnp.float32),
            pltpu.VMEM((CHUNKS, PLANE) + tiles, jnp.float32),
            pltpu.VMEM((4, 4, 128, 128), jnp.float32),
            pltpu.VMEM((CHUNKS, NZ, 8, 128), jnp.float32),
            dma, dma, dma, dma, dma((2,)), dma((2,)),
            dma((CHUNKS,)), dma((CHUNKS, PLANE)),
            dma((CHUNKS, 2)), dma((CHUNKS, 2)),
            dma((CHUNKS,)), dma((CHUNKS,)),
            dma((CHUNKS,)), dma((CHUNKS,)),
        ],
        compiler_params=pltpu.CompilerParams(
            collective_id=0, has_side_effects=True, vmem_limit_bytes=55500000
        ),
    )(psi.reshape(parts, cx, by, nz, orbs), potential.reshape(cx, by, nz))
    return result.reshape(psi.shape)


def solution(mesh):
    names = ("dom_0", "dom_1", "dom_2", "st")
    torus = Mesh(mesh.devices.reshape(NZ, NY, NX, mesh.shape["st"]), names)
    placed = (P(None, names[:3], None, None, None, "st"), P(names[:3], None, None, None))
    return jax.shard_map(
        on_device,
        mesh=torus,
        in_specs=placed,
        out_specs=P(None, names[:3], None, None, None, "st"),
        check_vma=False,
    )
```

time: 49.6 us -> 44.9 us (0.905)
  Pallas kernels: 46.4 us -> 42.7 us
  local copies, waits for them, and re-layouts: 2.89 us -> 1.67 us
    pallas_call x1, Pallas kernels: 46.4 us -> 42.7 us  [on_device(): pl.pallas_call(kernel, out_shape=jax.ShapeDtypeStruct((parts, cx, by, nz,...]
    unnamed x5 -> x3, local copies, waits for them, and re-layouts: 2.89 us -> 1.67 us
where the time goes in v4:
time: 44.9 us; the launch traced here: 44.4 us
  Pallas kernels  42.7 us (95%)
  local copies, waits for them, and re-layouts  1.67 us (4%)
    pallas_call x1, Pallas kernels, on_device(): pl.pallas_call(kernel, out_shape=jax.ShapeDtypeStruct((parts, cx, by, nz,...  42.7 us
    unnamed x3, local copies, waits for them, and re-layouts  1.67 us

profile of v4, /device:TPU:8, one launch (start us, length us, event | category | flops | bytes accessed | tf_op | source)
XLA Modules:
  0.0 44.4 jit_solution(3785262820153189291)
XLA Ops:
  0.0 0.0 copy-start
  0.0 0.7 %copy-done = f32[1,8,2,64]{3,2,1,0:T(2,128)S(1)} copy-done((f32[1,8,2,64]{3,2,1,0:T(2,128)S(1)}, f32[1,8,2,64]{3,2,1,0:T(2,128)}, u32[]{:S(2)}) %copy-start) | copy-done | bytes 4120
  0.7 42.7 %shard_map.28 = f32[2,8,2,64,128]{4,3,2,1,0:T(8,128)S(1)} custom-call(f32[2,8,2,64,128]{4,3,2,1,0:T(8,128)} %bitcast.7, f32[8,2,64]{2,1,0:T(2,128)S(1)} %bitcast.6), custom_call_target="tpu_custom_call" | custom-call | tf_op jit(solution)/shard_map/pallas_call | solution.py:486
  43.4 1.0 %copy.5 = f32[2,1,8,2,64,128]{5,4,3,2,1,0:T(8,128)} copy(f32[2,1,8,2,64,128]{5,4,3,2,1,0:T(8,128)S(1)} %bitcast.5) | data formatting | bytes 2097152
Async XLA Ops:
  0.0 0.7 %copy-start = (f32[1,8,2,64]{3,2,1,0:T(2,128)S(1)}, f32[1,8,2,64]{3,2,1,0:T(2,128)}, u32[]{:S(2)}) copy-start(f32[1,8,2,64]{3,2,1,0:T(2,128)} %param.3) | copy-start | bytes 12292

commit v5 on v4

--- a/solution.py
+++ b/solution.py
@@ -17,9 +17,10 @@
 NX, NY, NZ = 4, 4, 8
 PLANE = NX * NY
 SLABS = PLANE + 2 * HALO
+PAIR = 2
 CHUNKS = 4
 ORBS = 2
-GROUP = 8
+GROUP = 4
 OFFSETS = (
     (2, 2), (2, 1), (1, 2), (2, 3), (3, 2), (1, 1), (3, 3), (1, 3), (3, 1),
     (2, 0), (0, 2), (1, 0), (0, 1), (3, 0), (0, 3),
@@ -160,14 +161,14 @@
                 snd[chunk, :, i] = merged(tiles, chunk).T.reshape(PLANE, 8, 128)
 
     def rows(slab, count=1):
-        return pl.ds(pl.multiple_of(8 * slab, 8), 8 * count)
+        return pl.ds(8 * slab if isinstance(slab, int) else pl.multiple_of(8 * slab, 8), 8 * count)
 
     def send_in(chunk):
         for number, offset in enumerate(OFFSETS):
             peer, where = at(offset)
             pltpu.make_async_remote_copy(
                 src_ref=snd.at[chunk, peer], dst_ref=u0.at[chunk, :, rows(HALO + me)],
-                send_sem=in_send.at[chunk], recv_sem=in_recv.at[chunk, me],
+                send_sem=in_send, recv_sem=in_recv.at[chunk, number // PAIR],
                 device_id=where, device_id_type=MESH,
             ).start()
 
@@ -219,7 +220,7 @@
         target = p + HALO - PLANE if up else p + HALO + PLANE
         return pltpu.make_async_remote_copy(
             src_ref=u0.at[chunk, :, rows(HALO + p)], dst_ref=u0.at[chunk, :, rows(target)],
-            send_sem=halo_send.at[chunk, int(up)], recv_sem=halo_recv.at[chunk, int(up)],
+            send_sem=halo_send.at[int(up)], recv_sem=halo_recv.at[chunk, int(up)],
             device_id=above if up else below, device_id_type=MESH,
         )
 
@@ -243,10 +244,11 @@
 
     def forward(chunk):
         pass_on(chunk, me)
-        for offset in OFFSETS:
-            p = at((NY - offset[0], NX - offset[1]))[0]
-            wait_recv(u0.at[chunk, :, rows(HALO)], in_recv.at[chunk, p])
-            pass_on(chunk, p)
+        for first in range(0, len(OFFSETS), PAIR):
+            some = OFFSETS[first : first + PAIR]
+            wait_recv(u0.at[chunk, :, rows(HALO, len(some))], in_recv.at[chunk, first // PAIR])
+            for offset in some:
+                pass_on(chunk, at((NY - offset[0], NX - offset[1]))[0])
 
     wait_recv(pots.at[pl.ds(0, PLANE - 1)], pot_recv)
 
@@ -363,7 +365,7 @@
         for dz in range(1, NZ):
             pltpu.make_async_remote_copy(
                 src_ref=gram.at[chunk, z], dst_ref=gram.at[chunk, z],
-                send_sem=gram_send.at[chunk], recv_sem=gram_recv.at[chunk],
+                send_sem=gram_send, recv_sem=gram_recv.at[chunk],
                 device_id=(lax.rem(z + dz, NZ), y, x, st), device_id_type=MESH,
             ).start()
 
@@ -401,7 +403,7 @@
             peer, where = at(offset)
             pltpu.make_async_remote_copy(
                 src_ref=outs.at[chunk, peer], dst_ref=back.at[chunk, me],
-                send_sem=out_send.at[chunk], recv_sem=out_recv.at[chunk],
+                send_sem=out_send, recv_sem=out_recv.at[chunk],
                 device_id=where, device_id_type=MESH,
             ).start()
 
@@ -435,33 +437,35 @@
 
     set_centre(0, HALO)
     set_centre(HALO + PLANE, HALO)
-    for chunk in range(CHUNKS):
-        if 1 <= chunk < CHUNKS - 1:
-            forward(chunk + 1)
+    def close(chunk, inner):
         wait_halo(chunk)
-        gram[chunk, z] = advance(chunk + 1 if chunk + 1 < CHUNKS else None, chunk)
+        gram[chunk, z] = advance(inner, chunk)
         send_gram(chunk)
-        if chunk == CHUNKS - 2:
-            finish(0)
+
+    close(0, 1)
+    forward(2)
+    close(1, 2)
+    forward(3)
+    advance(3, None)
+    close(2, None)
+    finish(0)
+    close(3, None)
     for chunk in range(1, CHUNKS):
         finish(chunk)
 
     wait_send(pots.at[pl.ds(0, PLANE - 1)], pot_send)
-    for chunk in range(CHUNKS):
-        wait_send(snd.at[chunk, pl.ds(0, PLANE - 1)], in_send.at[chunk])
-        wait_send(gram.at[chunk, pl.ds(0, NZ - 1)], gram_send.at[chunk])
+    wait_send(snd.at[:, pl.ds(0, PLANE - 1)], in_send)
+    wait_send(gram.at[:, pl.ds(0, NZ - 1)], gram_send)
 
     @pl.when(has_low)
     def _():
         pot_halo_copy(False).wait_send()
-        for chunk in range(CHUNKS):
-            wait_send(u0.at[chunk, :, rows(0, HALO)], halo_send.at[chunk, 0])
+        wait_send(u0.at[:, :, rows(0, HALO)], halo_send.at[0])
 
     @pl.when(has_high)
     def _():
         pot_halo_copy(True).wait_send()
-        for chunk in range(CHUNKS):
-            wait_send(u0.at[chunk, :, rows(0, HALO)], halo_send.at[chunk, 1])
+        wait_send(u0.at[:, :, rows(0, HALO)], halo_send.at[1])
 
     for chunk in range(CHUNKS):
         wait_recv(back.at[chunk, pl.ds(0, PLANE - 1)], out_recv.at[chunk])
@@ -475,8 +479,7 @@
                 else:
                     out[g % 2, i, g // 2] = whole[0:64]
                     out[g % 2, i + 4, g // 2] = whole[64:128]
-    for chunk in range(CHUNKS):
-        wait_send(outs.at[chunk, pl.ds(0, PLANE - 1)], out_send.at[chunk])
+    wait_send(outs.at[:, pl.ds(0, PLANE - 1)], out_send)
 
 
 def on_device(psi, potential):
@@ -504,10 +507,10 @@
             pltpu.VMEM((4, 4, 128, 128), jnp.float32),
             pltpu.VMEM((CHUNKS, NZ, 8, 128), jnp.float32),
             dma, dma, dma, dma, dma((2,)), dma((2,)),
-            dma((CHUNKS,)), dma((CHUNKS, PLANE)),
-            dma((CHUNKS, 2)), dma((CHUNKS, 2)),
-            dma((CHUNKS,)), dma((CHUNKS,)),
-            dma((CHUNKS,)), dma((CHUNKS,)),
+            dma, dma((CHUNKS, -(-len(OFFSETS) // PAIR))),
+            dma((2,)), dma((CHUNKS, 2)),
+            dma, dma((CHUNKS,)),
+            dma, dma((CHUNKS,)),
         ],
         compiler_params=pltpu.CompilerParams(
             collective_id=0, has_side_effects=True, vmem_limit_bytes=55500000

time: 44.9 us -> 44.1 us (0.982)
  Pallas kernels: 42.7 us -> 41.9 us
    pallas_call x1, Pallas kernels: 42.7 us -> 41.9 us  [on_device(): pl.pallas_call(kernel, out_shape=jax.ShapeDtypeStruct((parts, cx, by, nz,...]
where the time goes in v5:
time: 44.1 us; the launch traced here: 43.6 us
  Pallas kernels  41.9 us (95%)
  local copies, waits for them, and re-layouts  1.67 us (4%)
    pallas_call x1, Pallas kernels, on_device(): pl.pallas_call(kernel, out_shape=jax.ShapeDtypeStruct((parts, cx, by, nz,...  41.9 us
    unnamed x3, local copies, waits for them, and re-layouts  1.67 us

profile of v5, /device:TPU:8, one launch (start us, length us, event | category | flops | bytes accessed | tf_op | source)
XLA Modules:
  0.0 43.6 jit_solution(6592519508669608851)
XLA Ops:
  0.0 0.0 copy-start
  0.0 0.7 %copy-done = f32[1,8,2,64]{3,2,1,0:T(2,128)S(1)} copy-done((f32[1,8,2,64]{3,2,1,0:T(2,128)S(1)}, f32[1,8,2,64]{3,2,1,0:T(2,128)}, u32[]{:S(2)}) %copy-start) | copy-done | bytes 4120
  0.7 41.9 %shard_map.28 = f32[2,8,2,64,128]{4,3,2,1,0:T(8,128)S(1)} custom-call(f32[2,8,2,64,128]{4,3,2,1,0:T(8,128)} %bitcast.7, f32[8,2,64]{2,1,0:T(2,128)S(1)} %bitcast.6), custom_call_target="tpu_custom_call" | custom-call | tf_op jit(solution)/shard_map/pallas_call | solution.py:489
  42.6 1.0 %copy.5 = f32[2,1,8,2,64,128]{5,4,3,2,1,0:T(8,128)} copy(f32[2,1,8,2,64,128]{5,4,3,2,1,0:T(8,128)S(1)} %bitcast.5) | data formatting | bytes 2097152
Async XLA Ops:
  0.0 0.7 %copy-start = (f32[1,8,2,64]{3,2,1,0:T(2,128)S(1)}, f32[1,8,2,64]{3,2,1,0:T(2,128)}, u32[]{:S(2)}) copy-start(f32[1,8,2,64]{3,2,1,0:T(2,128)} %param.3) | copy-start | bytes 12292
